TPU v7x, 32 devices: a whole 2x2x4 slice. The times are simulated.
32 devices in a mesh: row: 2 (over core), col: 16 (over z, y, x).
Axes of the slice: x: 2, y: 2, z: 4, core: 2. Of those that a mesh axis runs over, the one named last changes fastest.
Arguments:
- movie: bfloat16 [128, 1024, 256], P('row', 'col'), may hold values from 0 to 1.5
- footprints: float32 [2, 16, 12, 4096], P('row', 'col'), may hold values from 0.05 to 1
- anchors: int32 [2, 16, 12, 2], P('row', 'col'), may hold values from 0 to 63, as said below
- groups: int32 [2, 16, 12], P('row', 'col'), may hold values from 0 to 3, as said below
- counts: int32 [2, 16], P('row', 'col'), may hold values from 1 to 12, as said below
- temporal: float32 [2, 16, 12, 256], P('row', 'col'), may hold values from 0.2 to 2
- back_spatial: bfloat16 [2, 128, 1024], P(None, 'row', 'col'), may hold values from 0 to 0.5
- back_temporal: float32 [2, 256], replicated, may hold values from 0.5 to 1
- window: int32 [2], replicated, may hold values from 0 to 256, as said below
Outputs:
- new_footprints: float32 [2, 16, 12, 4096], P('row', 'col')
- new_traces: float32 [2, 16, 12, 256], P('row', 'col')
Inputs may be any that keep to these rules, and one draw needn't show every extreme that they name: `anchors`: a block's anchor lies in its tile; on the last tile row the row offset is at most 0, on the last tile column the column offset at most 0. `counts`: slots below the count are live, the others are ignored; some tile has 12 live slots. `groups`: every tile has exactly 3 slots, live or not, in each group. window[0] is at most 64 and window[1] at least 192.
All inputs are finite; a program needn't handle non-finite values.
Results may differ from a plain program's by a relative error of at most 0.00084.
Values may be sent and summed in bfloat16 or wider, within the bound.
No kernel may reach another device: no remote copies, remote signals or barrier semaphores. Data moves between devices by JAX's collectives and lax.ppermute only.
A program may use at most 64 MiB of HBM per device.

v0:
```python
import jax
import jax.numpy as jnp
from jax import lax
from jax.sharding import PartitionSpec as P

FP = 64
GROUPS = 4


exact_mode = lax.Precision.HIGHEST


def padded(cells, sides, width):
    for axis, dim in sides:
        count = lax.axis_size(axis)
        ends = count - 1
        head = lax.slice_in_dim(cells, 0, width, axis=dim)
        tail = lax.slice_in_dim(cells, cells.shape[dim] - width, cells.shape[dim], axis=dim)
        cells = jnp.concatenate(
            [
                lax.ppermute(tail, axis, [(i, (i + 1) % count) for i in range(ends)]),
                cells,
                lax.ppermute(head, axis, [((i + 1) % count, i) for i in range(ends)]),
            ],
            axis=dim,
        )
    return cells


def shifted(value, axis, steps):
    count = lax.axis_size(axis)
    initial, last = (max(0, -steps), min(count, count - steps))
    return lax.ppermute(value, axis, [(source, source + steps) for source in range(initial, last)])


def near_traces(traces):
    return padded(traces[None, None], (("row", 0), ("col", 1)), 1)


def selector(starts, extent):
    places = jnp.arange(extent, dtype=jnp.int32)[None, :, None]
    offsets = jnp.arange(FP, dtype=jnp.int32)[None, None, :]
    return (places == starts[:, None, None] + offsets).astype(jnp.float32)


def on_device(
    movie, footprints, anchors, groups, counts, temporal, back_spatial, back_temporal, window
):
    tile_rows, tile_cols, frame_count = movie.shape
    slot_count = footprints.shape[2]
    pixels = tile_rows * tile_cols
    ext_rows = tile_rows + FP
    ext_cols = tile_cols + FP
    ext_pixels = ext_rows * ext_cols
    count_near = 9 * slot_count
    count_tile = 4 * slot_count
    slot_ids = jnp.arange(slot_count, dtype=jnp.int32)
    living = (slot_ids < counts[0, 0]).astype(jnp.float32)
    shapes = footprints[0, 0] * living[:, None]
    labels = jnp.concatenate(
        [
            anchors[0, 0].astype(jnp.float32),
            groups[0, 0][:, None].astype(jnp.float32),
            living[:, None],
        ],
        axis=1,
    )
    near_shapes, near_labels = (
        padded(shapes[None, None], (("row", 0), ("col", 1)), 1),
        padded(labels[None, None], (("row", 0), ("col", 1)), 1),
    )
    tile_step = jnp.arange(3, dtype=jnp.int32) - 1
    top_rows = (
        near_labels[..., 0].astype(jnp.int32) + (tile_step * tile_rows)[:, None, None]
    ).reshape(count_near)
    left_cols = (
        near_labels[..., 1].astype(jnp.int32) + (tile_step * tile_cols)[None, :, None]
    ).reshape(count_near)
    near_groups = near_labels[..., 2].astype(jnp.int32)
    tile_groups = near_groups[:2, :2].reshape(count_tile)
    tile_living = near_labels[:2, :2, :, 3].reshape(count_tile)
    row_pick = selector(top_rows, ext_rows)
    col_pick = selector(left_cols, ext_cols)
    sectioned = jnp.einsum(
        "nyi,nij->nyj", row_pick, near_shapes.reshape(count_near, FP, FP), precision=exact_mode
    )
    canvas = jnp.einsum("nyj,nxj->nyx", sectioned, col_pick, precision=exact_mode)
    flattened = canvas.reshape(count_near, ext_pixels)
    owned = flattened[4 * slot_count : 5 * slot_count]
    coupling = jnp.dot(owned, flattened.T, precision=exact_mode)
    self_weight = jnp.diagonal(coupling[:, 4 * slot_count : 5 * slot_count])
    safe_self = jnp.where(living > 0, self_weight, 1.0)
    tile_canvas = canvas.reshape(3, 3, slot_count, ext_rows, ext_cols)[
        :2, :2, :, :tile_rows, :tile_cols
    ].reshape(count_tile, pixels)
    row_select = row_pick.reshape(3, 3, slot_count, ext_rows, FP)[:2, :2, :, :tile_rows].reshape(
        count_tile, tile_rows, FP
    )
    col_select = col_pick.reshape(3, 3, slot_count, ext_cols, FP)[:2, :2, :, :tile_cols].reshape(
        count_tile, tile_cols, FP
    )
    back_tile = back_spatial.astype(jnp.float32).reshape(2, pixels)
    movie_flat = movie.reshape(pixels, frame_count)
    loadings = jnp.dot(tile_canvas, back_tile.T, precision=exact_mode)
    shares = jnp.dot(
        tile_canvas.astype(jnp.bfloat16), movie_flat, preferred_element_type=jnp.float32
    )
    shares = (shares - jnp.dot(loadings, back_temporal, precision=exact_mode)).reshape(
        2, 2, slot_count, frame_count
    )
    from_east = shifted(shares[:, 0], "col", -1)
    column_sum = shares[:, 1] + from_east
    from_south = shifted(column_sum[0], "row", -1)
    drives = column_sum[1] + from_south
    moments = jnp.arange(frame_count, dtype=jnp.int32)
    inside = ((moments >= window[0]) & (moments < window[1])).astype(jnp.float32)
    row_cover = jnp.sum(row_select, axis=2)
    col_cover = jnp.sum(col_select, axis=2)
    cover = (row_cover[:, :, None] * col_cover[:, None, :]).reshape(
        count_tile, pixels
    ) * tile_living[:, None]
    traces = temporal[0, 0]
    nearby = near_traces(traces)
    first_near = nearby
    for step in range(GROUPS):
        if step > 0:
            nearby = near_traces(traces)
        temporal_coupled = jnp.dot(
            coupling, nearby.reshape(count_near, frame_count), precision=exact_mode
        )
        temporal_chosen = living * (groups[0, 0] == step).astype(jnp.float32)
        temporal_updated = jnp.maximum(
            traces + (drives - temporal_coupled) / safe_self[:, None], 0.0
        )
        traces = jnp.where(temporal_chosen[:, None] > 0, temporal_updated, traces)
    tile_traces = first_near[:2, :2].reshape(count_tile, frame_count)
    weighted = tile_traces * inside[None, :]
    intersection_time = jnp.dot(weighted, weighted.T, precision=exact_mode)
    safe_mass = jnp.where(tile_living > 0, jnp.diagonal(intersection_time), 1.0)
    back_loads = jnp.dot(weighted, back_temporal.T, precision=exact_mode)
    target = lax.dot_general(
        weighted.astype(jnp.bfloat16),
        movie_flat,
        (((1,), (1,)), ((), ())),
        preferred_element_type=jnp.float32,
    )
    target = target - jnp.dot(back_loads, back_tile, precision=exact_mode)
    values = tile_canvas
    for step in range(GROUPS):
        coupled = jnp.dot(intersection_time, values, precision=exact_mode)
        chosen = cover * (tile_groups == step).astype(jnp.float32)[:, None]
        updated = jnp.maximum(values + (target - coupled) / safe_mass[:, None], 0.0)
        values = jnp.where(chosen > 0, updated, values)
    lifted = jnp.einsum(
        "nyi,nyx->nix",
        row_select,
        values.reshape(count_tile, tile_rows, tile_cols),
        precision=exact_mode,
    )
    blocks = jnp.einsum("nix,nxj->nij", lifted, col_select, precision=exact_mode).reshape(
        2, 2, slot_count, FP * FP
    )
    from_east = shifted(blocks[:, 0], "col", -1)
    column_sum = blocks[:, 1] + from_east
    from_south = shifted(column_sum[0], "row", -1)
    new_shapes = column_sum[1] + from_south
    return (new_shapes[None, None], traces[None, None])


def solution(mesh):
    return jax.shard_map(
        on_device,
        mesh=mesh,
        in_specs=(
            P("row", "col", None),
            P("row", "col", None, None),
            P("row", "col", None, None),
            P("row", "col", None),
            P("row", "col"),
            P("row", "col", None, None),
            P(None, "row", "col"),
            P(),
            P(),
        ),
        out_specs=(P("row", "col", None, None), P("row", "col", None, None)),
        check_vma=False,
    )
```

profile of v0, /device:TPU:17, one launch (start us, length us, event | category | flops | bytes accessed | tf_op | source)
XLA Modules:
  0.0 199.4 jit_solution(4359725919975137092)
XLA Ops:
  2.8 1.3 collective-permute-start
  4.1 3.0 %collective-permute-start.1 = (f32[1,1,12,4]{2,3,1,0:T(4,128)S(1)}, f32[1,1,12,4]{2,3,1,0:T(4,128)S(1)}, u32[]{:S(2)}, u32[]{:S(2)}) collective-permute-start(f32[1,1,12,4]{2,3,1,0:T(4,128)S(1)} %maximum_bitcast_fusion), channel_id=1, source_target_pairs={{16,0},{17,1},{18,2},{19,3},{20,4},{21,5},{22,6},{23,7},{24,8},{25... | collective-permute-start | bytes 584 | tf_op jit(solution)/shard_map/ppermute | solution.py:23
  7.2 1.1 broadcast_multiply_fusion.1
  8.3 1.3 collective-permute-start.4
  9.6 3.0 %collective-permute-start.5 = (f32[1,1,12,4096]{3,1,2,0:T(1,128)S(1)}, f32[1,1,12,4096]{3,1,2,0:T(1,128)S(1)}, u32[]{:S(2)}, u32[]{:S(2)}) collective-permute-start(f32[1,1,12,4096]{3,1,2,0:T(1,128)S(1)} %broadcast_multiply_fusion.1), channel_id=1, source_target_pairs={{16,0},{17,1},{18,2},{19,3},{20,4},{21,5},{22,6},{23,7},{24,8},{25... | collective-permute-start | bytes 589832 | tf_op jit(solution)/shard_map/ppermute | solution.py:23
  12.7 1.3 collective-permute-start.8
  14.0 1.2 fusion.53
  15.2 1.3 fusion.60
  16.5 1.2 and_convert_fusion
  17.8 3.1 %collective-permute-start.2 = (f32[3,1,12,4]{2,3,1,0:T(4,128)S(1)}, f32[3,1,12,4]{2,3,1,0:T(4,128)S(1)}, u32[]{:S(2)}, u32[]{:S(2)}) collective-permute-start(f32[3,1,12,4]{2,3,1,0:T(4,128)S(1)} %pad_maximum_fusion.10), channel_id=1, source_target_pairs={{0,1},{1,2},{2,3},{3,4},{4,5},{5,6},{6,7},{7,8},{8,9},{9,10},{10,1... | collective-permute-start | bytes 1736 | tf_op jit(solution)/shard_map/ppermute | solution.py:21
  20.9 4.0 %collective-permute-start.3 = (f32[3,1,12,4]{2,3,1,0:T(4,128)S(1)}, f32[3,1,12,4]{2,3,1,0:T(4,128)S(1)}, u32[]{:S(2)}, u32[]{:S(2)}) collective-permute-start(f32[3,1,12,4]{2,3,1,0:T(4,128)S(1)} %pad_maximum_fusion.10), channel_id=1, source_target_pairs={{1,0},{2,1},{3,2},{4,3},{5,4},{6,5},{7,6},{8,7},{9,8},{10,9},{11,1... | collective-permute-start | bytes 1736 | tf_op jit(solution)/shard_map/ppermute | solution.py:23
  25.2 0.9 reshape.333
  26.1 3.6 %collective-permute-start.9 = (f32[1,1,12,256]{3,1,2,0:T(1,128)}, f32[1,1,12,256]{3,1,2,0:T(1,128)S(1)}, u32[]{:S(2)}, u32[]{:S(2)}) collective-permute-start(f32[1,1,12,256]{3,1,2,0:T(1,128)} %param.14), channel_id=1, source_target_pairs={{16,0},{17,1},{18,2},{19,3},{20,4},{21,5},{22,6},{23,7},{24,8},{25... | collective-permute-start | bytes 36872 | tf_op jit(solution)/shard_map/ppermute | solution.py:23
  30.5 1.3 add_compare_fusion.1
  33.5 1.7 broadcast_multiply_fusion
  35.3 1.9 collective-permute-start.10
  37.2 2.8 %mul.125 = f32[48,4096]{1,0:T(8,128)} reshape(f32[48,64,64]{2,1,0:T(8,128)} %broadcast_multiply_fusion) | data formatting | bytes 1572864 | tf_op jit(solution)/shard_map/mul | solution.py:119
  42.7 5.1 %collective-permute-start.15 = (f32[3,1,12,256]{3,1,2,0:T(1,128)S(1)}, f32[3,1,12,256]{3,1,2,0:T(1,128)S(1)}, u32[]{:S(2)}, u32[]{:S(2)}) collective-permute-start(f32[3,1,12,256]{3,1,2,0:T(1,128)S(1)} %constant_dynamic-update-slice_fusion), channel_id=1, source_target_pairs={{1,0},{2,1},{3,2},{4,3},{5,4},{6,5},{7,6},{8,7},{9,8},{10,9},{11,1... | collective-permute-start | bytes 110600 | tf_op jit(solution)/shard_map/ppermute | solution.py:23
  48.1 1.0 gather_fusion
  49.8 1.4 pad_maximum_fusion.1
  51.2 1.9 collective-permute-start.6
  53.2 5.2 %collective-permute-start.7 = (f32[3,1,12,4096]{3,1,2,0:T(1,128)}, f32[3,1,12,4096]{3,1,2,0:T(1,128)}, u32[]{:S(2)}, u32[]{:S(2)}) collective-permute-start(f32[3,1,12,4096]{3,1,2,0:T(1,128)} %pad_maximum_fusion.1), channel_id=1, source_target_pairs={{1,0},{2,1},{3,2},{4,3},{5,4},{6,5},{7,6},{8,7},{9,8},{10,9},{11,1... | collective-permute-start | bytes 1769480 | tf_op jit(solution)/shard_map/ppermute | solution.py:23
  59.9 1.4 convolution_subtract_fusion.4
  61.3 17.8 %collective-permute-done.6 = f32[3,1,12,4096]{3,1,2,0:T(1,128)} collective-permute-done((f32[3,1,12,4096]{3,1,2,0:T(1,128)}, f32[3,1,12,4096]{3,1,2,0:T(1,128)}, u32[]{:S(2)}, u32[]{:S(2)}) %collective-permute-start.6) | collective-permute-done | bytes 589856 | tf_op jit(solution)/shard_map/ppermute | solution.py:21
  79.1 1.0 collective-permute-done.7
  80.1 2.8 %pad_maximum_fusion = f32[3,3,12,4096]{3,1,2,0:T(4,128)S(1)} fusion(f32[3,1,12,4096]{3,1,2,0:T(1,128)} %collective-permute-done.7, f32[1,1,12,4096]{3,1,2,0:T(1,128)S(1)} %collective-permute-done.5, f32[1,1,12,4096]{3,1,2,0:T(1,128)S(1)} %broadcast_multiply_fusion.1, f32[1,1,12,4096]{3,1,2,0:T(1,128)S(1)} %collective-permute-done.4, ...), kind=kLoop, calls=%fused_computation.29 | loop fusion | flops 1769472 | bytes 3538944 | tf_op jit(solution)/shard_map/concatenate | solution.py:19
  83.0 2.5 %copy.31 = f32[3,3,12,4096]{3,2,1,0:T(8,128)} copy(f32[3,3,12,4096]{3,1,2,0:T(4,128)S(1)} %pad_maximum_fusion) | data formatting | bytes 3538944 | tf_op jit(solution)/shard_map/concatenate | solution.py:19
  85.5 4.0 %reshape.328 = f32[108,64,64]{2,1,0:T(8,128)} reshape(f32[3,3,12,4096]{3,2,1,0:T(8,128)} %copy.31) | data formatting | bytes 3538944 | tf_op jit(solution)/shard_map/reshape | solution.py:85
  89.4 6.6 %fusion.18 = f32[108,128,64]{1,2,0:T(8,128)S(1)} fusion(f32[108,64,64]{2,1,0:T(8,128)} %reshape.328, s32[108,64]{1,0:T(8,128)S(1)} %copy-done.7), kind=kOutput, calls=%fused_computation.27 | convolution fusion | flops 680361984 | bytes 5336064 | tf_op jit(solution)/shard_map/nyi,nij->nyj/dot_general | solution.py:84
  96.0 7.5 %fusion.19 = f32[108,128,128]{2,1,0:T(8,128)S(1)} fusion(f32[108,128,64]{1,2,0:T(8,128)S(1)} %fusion.18, s32[108,64]{1,0:T(8,128)S(1)} %iota_add_fusion.2), kind=kOutput, calls=%fused_computation.28 | convolution fusion | flops 1359839232 | bytes 10644480 | tf_op jit(solution)/shard_map/nyj,nxj->nyx/dot_general | solution.py:87
  103.6 1.3 slice.102
  105.0 9.0 %fusion.39 = f32[12,108]{1,0:T(8,128)S(1)} fusion(f32[108,128,128]{2,1,0:T(8,128)S(1)} %fusion.19, f32[12,128,128]{2,1,0:T(8,128)S(1)} %slice.111), kind=kOutput, calls=%fused_computation.58 | convolution fusion | flops 254803968 | bytes 7869504 | tf_op jit(solution)/shard_map/dot_general | solution.py:90
  114.0 2.8 %reshape.330 = f32[48,4096]{1,0:T(8,128)} reshape(f32[2,2,12,64,64]{4,3,2,1,0:T(8,128)} %slice.102) | data formatting | bytes 1572864 | tf_op jit(solution)/shard_map/reshape | solution.py:95
  116.8 1.6 fusion.66
  118.4 1.4 convert_element_type.176
  119.8 1.5 fusion.65
  121.6 4.5 %collective-permute-start.13 = (f32[2,12,256]{2,1,0:T(8,128)S(1)}, f32[2,12,256]{2,1,0:T(8,128)S(1)}, u32[]{:S(2)}, u32[]{:S(2)}) collective-permute-start(f32[2,12,256]{2,1,0:T(8,128)S(1)} %slice_bitcast_fusion.4), channel_id=1, source_target_pairs={{1,0},{2,1},{3,2},{4,3},{5,4},{6,5},{7,6},{8,7},{9,8},{10,9},{11,1... | collective-permute-start | bytes 73736 | tf_op jit(solution)/shard_map/ppermute | solution.py:33
  126.1 2.3 %fusion.5 = f32[48,4096]{1,0:T(8,128)S(1)} fusion(f32[48,4096]{1,0:T(8,128)S(1)} %copy-done.1, f32[48,4096]{1,0:T(8,128)} %convolution_subtract_fusion.4, f32[48,48]{1,0:T(8,128)S(1)} %fusion.62, f32[48,4096]{1,0:T(8,128)} %mul.125, f32[48]{0:T(128)S(1)} %copy-done.21, f32[48]{0:T(128)S(1)} %copy-done.18, f32[48]{0:T(128)S(1)} %copy-done.16), kind=kOutput, calls=%fused_computation.11 | convolution fusion | flops 114819072 | bytes 3155520 | tf_op jit(solution)/shard_map/dot_general | solution.py:150
  128.5 0.9 fusion.9
  129.5 1.8 fusion.13
  132.2 2.6 %collective-permute-start.14 = (f32[12,256]{1,0:T(8,128)S(1)}, f32[12,256]{1,0:T(8,128)S(1)}, u32[]{:S(2)}, u32[]{:S(2)}) collective-permute-start(f32[12,256]{1,0:T(8,128)S(1)} %slice_bitcast_fusion.6), channel_id=1, source_target_pairs={{16,0},{17,1},{18,2},{19,3},{20,4},{21,5},{22,6},{23,7},{24,8},{25... | collective-permute-start | bytes 36872 | tf_op jit(solution)/shard_map/ppermute | solution.py:33
  135.8 1.3 collective-permute-start.16
  137.1 3.0 %collective-permute-start.17 = (f32[1,1,12,256]{3,2,1,0:T(8,128)S(1)}, f32[1,1,12,256]{3,2,1,0:T(8,128)S(1)}, u32[]{:S(2)}, u32[]{:S(2)}) collective-permute-start(f32[1,1,12,256]{3,2,1,0:T(8,128)S(1)} %bitcast.137), channel_id=1, source_target_pairs={{16,0},{17,1},{18,2},{19,3},{20,4},{21,5},{22,6},{23,7},{24,8},{25... | collective-permute-start | bytes 36872 | tf_op jit(solution)/shard_map/ppermute | solution.py:23
  140.2 3.7 %fusion.17 = f32[48,4096]{1,0:T(8,128)} fusion(f32[48,4096]{1,0:T(8,128)} %fusion.13, f32[48,4096]{1,0:T(8,128)} %convolution_subtract_fusion.4, f32[48,48]{1,0:T(8,128)S(1)} %fusion.62, f32[48,4096]{1,0:T(8,128)} %mul.125, f32[48]{0:T(128)S(1)} %copy-done.21, f32[48]{0:T(128)S(1)} %copy-done.17, f32[48]{0:T(128)S(1)} %copy-done.16), kind=kOutput, calls=%fused_computation.23 | convolution fusion | flops 114819072 | bytes 3155520 | tf_op jit(solution)/shard_map/dot_general | solution.py:150
  143.8 3.0 %reshape.334 = f32[48,64,64]{2,1,0:T(8,128)} reshape(f32[48,4096]{1,0:T(8,128)} %fusion.17) | data formatting | bytes 1572864 | tf_op jit(solution)/shard_map/reshape | solution.py:157
  146.9 1.9 collective-permute-start.18
  148.8 5.2 %collective-permute-start.19 = (f32[3,1,12,256]{3,2,1,0:T(8,128)S(1)}, f32[3,1,12,256]{3,2,1,0:T(8,128)S(1)}, u32[]{:S(2)}, u32[]{:S(2)}) collective-permute-start(f32[3,1,12,256]{3,2,1,0:T(8,128)S(1)} %pad_maximum_fusion.7), channel_id=1, source_target_pairs={{1,0},{2,1},{3,2},{4,3},{5,4},{6,5},{7,6},{8,7},{9,8},{10,9},{11,1... | collective-permute-start | bytes 110600 | tf_op jit(solution)/shard_map/ppermute | solution.py:23
  154.0 3.6 %fusion.63 = f32[48,64,64]{2,1,0:T(8,128)} fusion(pred[48,64,64]{1,2,0:T(32,128)(4,1)S(1)} %bitcast.131, f32[48,64,64]{2,1,0:T(8,128)} %reshape.334), kind=kOutput, calls=%fused_computation.144 | convolution fusion | flops 150994944 | bytes 1769472 | tf_op jit(solution)/shard_map/nyi,nyx->nix/dot_general | solution.py:154
  157.8 1.3 collective-permute-start.20
  159.1 3.0 %collective-permute-start.21 = (f32[1,1,12,256]{3,2,1,0:T(8,128)S(1)}, f32[1,1,12,256]{3,2,1,0:T(8,128)S(1)}, u32[]{:S(2)}, u32[]{:S(2)}) collective-permute-start(f32[1,1,12,256]{3,2,1,0:T(8,128)S(1)} %bitcast.141), channel_id=1, source_target_pairs={{16,0},{17,1},{18,2},{19,3},{20,4},{21,5},{22,6},{23,7},{24,8},{25... | collective-permute-start | bytes 36872 | tf_op jit(solution)/shard_map/ppermute | solution.py:23
  162.1 3.6 %fusion.64 = f32[48,64,64]{2,1,0:T(8,128)} fusion(f32[48,64,64]{2,1,0:T(8,128)} %fusion.63, pred[48,64,64]{2,1,0:T(32,128)(4,1)S(1)} %bitcast.130), kind=kOutput, calls=%fused_computation.145 | convolution fusion | flops 150994944 | bytes 1769472 | tf_op jit(solution)/shard_map/nix,nxj->nij/dot_general | solution.py:160
  165.7 1.9 reshape.336
  167.7 1.9 collective-permute-start.22
  169.6 5.2 %collective-permute-start.23 = (f32[3,1,12,256]{3,2,1,0:T(8,128)S(1)}, f32[3,1,12,256]{3,2,1,0:T(8,128)S(1)}, u32[]{:S(2)}, u32[]{:S(2)}) collective-permute-start(f32[3,1,12,256]{3,2,1,0:T(8,128)S(1)} %pad_maximum_fusion.8), channel_id=1, source_target_pairs={{1,0},{2,1},{3,2},{4,3},{5,4},{6,5},{7,6},{8,7},{9,8},{10,9},{11,1... | collective-permute-start | bytes 110600 | tf_op jit(solution)/shard_map/ppermute | solution.py:23
  175.6 1.9 collective-permute-start.11
  177.8 1.3 collective-permute-start.24
  179.1 3.0 %collective-permute-start.25 = (f32[1,1,12,256]{3,2,1,0:T(8,128)S(1)}, f32[1,1,12,256]{3,2,1,0:T(8,128)S(1)}, u32[]{:S(2)}, u32[]{:S(2)}) collective-permute-start(f32[1,1,12,256]{3,2,1,0:T(8,128)S(1)} %bitcast.133), channel_id=1, source_target_pairs={{16,0},{17,1},{18,2},{19,3},{20,4},{21,5},{22,6},{23,7},{24,8},{25... | collective-permute-start | bytes 36872 | tf_op jit(solution)/shard_map/ppermute | solution.py:23
  183.0 3.4 %collective-permute-start.26 = (f32[3,1,12,256]{3,2,1,0:T(8,128)S(1)}, f32[3,1,12,256]{3,2,1,0:T(8,128)S(1)}, u32[]{:S(2)}, u32[]{:S(2)}) collective-permute-start(f32[3,1,12,256]{3,2,1,0:T(8,128)S(1)} %pad_maximum_fusion.9), channel_id=1, source_target_pairs={{0,1},{1,2},{2,3},{3,4},{4,5},{5,6},{6,7},{7,8},{8,9},{9,10},{10,1... | collective-permute-start | bytes 110600 | tf_op jit(solution)/shard_map/ppermute | solution.py:21
  186.3 3.7 %collective-permute-start.27 = (f32[3,1,12,256]{3,2,1,0:T(8,128)S(1)}, f32[3,1,12,256]{3,2,1,0:T(8,128)S(1)}, u32[]{:S(2)}, u32[]{:S(2)}) collective-permute-start(f32[3,1,12,256]{3,2,1,0:T(8,128)S(1)} %pad_maximum_fusion.9), channel_id=1, source_target_pairs={{1,0},{2,1},{3,2},{4,3},{5,4},{6,5},{7,6},{8,7},{9,8},{10,9},{11,1... | collective-permute-start | bytes 110600 | tf_op jit(solution)/shard_map/ppermute | solution.py:23
  190.0 1.3 collective-permute-done.11
  191.4 1.1 fusion.43
  193.3 3.1 %collective-permute-start.12 = (f32[12,4096]{1,0:T(8,128)S(1)}, f32[12,4096]{1,0:T(8,128)S(1)}, u32[]{:S(2)}, u32[]{:S(2)}) collective-permute-start(f32[12,4096]{1,0:T(8,128)S(1)} %slice_bitcast_fusion.2), channel_id=1, source_target_pairs={{16,0},{17,1},{18,2},{19,3},{20,4},{21,5},{22,6},{23,7},{24,8},{25... | collective-permute-start | bytes 589832 | tf_op jit(solution)/shard_map/ppermute | solution.py:33
  197.5 1.0 fusion.45
  198.5 0.9 copy.42
  (151 shorter events, 15.6 us)
Async XLA Ops:
  0.6 58.5 %copy-start = (bf16[64,64,256]{2,1,0:T(8,128)(2,1)S(1)}, bf16[64,64,256]{2,1,0:T(8,128)(2,1)}, u32[]{:S(2)}) copy-start(bf16[64,64,256]{2,1,0:T(8,128)(2,1)} %param.9) | copy-start | bytes 6291460
  0.6 34.6 %copy-start.8 = (f32[1,1,12,256]{3,1,2,0:T(1,128)S(1)}, f32[1,1,12,256]{3,1,2,0:T(1,128)}, u32[]{:S(2)}) copy-start(f32[1,1,12,256]{3,1,2,0:T(1,128)} %param.14) | copy-start | bytes 36868
  2.8 14.9 %collective-permute-start = (f32[1,1,12,4]{2,3,1,0:T(4,128)S(1)}, f32[1,1,12,4]{2,3,1,0:T(4,128)S(1)}, u32[]{:S(2)}, u32[]{:S(2)}) collective-permute-start(f32[1,1,12,4]{2,3,1,0:T(4,128)S(1)} %maximum_bitcast_fusion), channel_id=1, source_target_pairs={{0,16},{1,17},{2,18},{3,19},{4,20},{5,21},{6,22},{7,23},{8,24},{9,... | collective-permute-start | bytes 584 | tf_op jit(solution)/shard_map/ppermute | solution.py:21
  4.1 13.6 %collective-permute-start.1 = (f32[1,1,12,4]{2,3,1,0:T(4,128)S(1)}, f32[1,1,12,4]{2,3,1,0:T(4,128)S(1)}, u32[]{:S(2)}, u32[]{:S(2)}) collective-permute-start(f32[1,1,12,4]{2,3,1,0:T(4,128)S(1)} %maximum_bitcast_fusion), channel_id=1, source_target_pairs={{16,0},{17,1},{18,2},{19,3},{20,4},{21,5},{22,6},{23,7},{24,8},{25... | collective-permute-start | bytes 584 | tf_op jit(solution)/shard_map/ppermute | solution.py:23
  8.3 41.5 %collective-permute-start.4 = (f32[1,1,12,4096]{3,1,2,0:T(1,128)S(1)}, f32[1,1,12,4096]{3,1,2,0:T(1,128)S(1)}, u32[]{:S(2)}, u32[]{:S(2)}) collective-permute-start(f32[1,1,12,4096]{3,1,2,0:T(1,128)S(1)} %broadcast_multiply_fusion.1), channel_id=1, source_target_pairs={{0,16},{1,17},{2,18},{3,19},{4,20},{5,21},{6,22},{7,23},{8,24},{9,... | collective-permute-start | bytes 589832 | tf_op jit(solution)/shard_map/ppermute | solution.py:21
  9.6 40.2 %collective-permute-start.5 = (f32[1,1,12,4096]{3,1,2,0:T(1,128)S(1)}, f32[1,1,12,4096]{3,1,2,0:T(1,128)S(1)}, u32[]{:S(2)}, u32[]{:S(2)}) collective-permute-start(f32[1,1,12,4096]{3,1,2,0:T(1,128)S(1)} %broadcast_multiply_fusion.1), channel_id=1, source_target_pairs={{16,0},{17,1},{18,2},{19,3},{20,4},{21,5},{22,6},{23,7},{24,8},{25... | collective-permute-start | bytes 589832 | tf_op jit(solution)/shard_map/ppermute | solution.py:23
  12.7 22.5 %collective-permute-start.8 = (f32[1,1,12,256]{3,1,2,0:T(1,128)}, f32[1,1,12,256]{3,1,2,0:T(1,128)S(1)}, u32[]{:S(2)}, u32[]{:S(2)}) collective-permute-start(f32[1,1,12,256]{3,1,2,0:T(1,128)} %param.14), channel_id=1, source_target_pairs={{0,16},{1,17},{2,18},{3,19},{4,20},{5,21},{6,22},{7,23},{8,24},{9,... | collective-permute-start | bytes 36872 | tf_op jit(solution)/shard_map/ppermute | solution.py:21
  17.8 8.3 %collective-permute-start.2 = (f32[3,1,12,4]{2,3,1,0:T(4,128)S(1)}, f32[3,1,12,4]{2,3,1,0:T(4,128)S(1)}, u32[]{:S(2)}, u32[]{:S(2)}) collective-permute-start(f32[3,1,12,4]{2,3,1,0:T(4,128)S(1)} %pad_maximum_fusion.10), channel_id=1, source_target_pairs={{0,1},{1,2},{2,3},{3,4},{4,5},{5,6},{6,7},{7,8},{8,9},{9,10},{10,1... | collective-permute-start | bytes 1736 | tf_op jit(solution)/shard_map/ppermute | solution.py:21
  20.9 8.8 %collective-permute-start.3 = (f32[3,1,12,4]{2,3,1,0:T(4,128)S(1)}, f32[3,1,12,4]{2,3,1,0:T(4,128)S(1)}, u32[]{:S(2)}, u32[]{:S(2)}) collective-permute-start(f32[3,1,12,4]{2,3,1,0:T(4,128)S(1)} %pad_maximum_fusion.10), channel_id=1, source_target_pairs={{1,0},{2,1},{3,2},{4,3},{5,4},{6,5},{7,6},{8,7},{9,8},{10,9},{11,1... | collective-permute-start | bytes 1736 | tf_op jit(solution)/shard_map/ppermute | solution.py:23
  26.1 9.2 %collective-permute-start.9 = (f32[1,1,12,256]{3,1,2,0:T(1,128)}, f32[1,1,12,256]{3,1,2,0:T(1,128)S(1)}, u32[]{:S(2)}, u32[]{:S(2)}) collective-permute-start(f32[1,1,12,256]{3,1,2,0:T(1,128)} %param.14), channel_id=1, source_target_pairs={{16,0},{17,1},{18,2},{19,3},{20,4},{21,5},{22,6},{23,7},{24,8},{25... | collective-permute-start | bytes 36872 | tf_op jit(solution)/shard_map/ppermute | solution.py:23
  35.2 13.9 %copy-start.10 = (f32[2,256]{1,0:T(2,128)S(1)}, f32[2,256]{1,0:T(2,128)}, u32[]{:S(2)}) copy-start(f32[2,256]{1,0:T(2,128)} %param.16) | copy-start | bytes 6148
  35.3 12.5 %collective-permute-start.10 = (f32[3,1,12,256]{3,1,2,0:T(1,128)S(1)}, f32[3,1,12,256]{3,1,2,0:T(1,128)S(1)}, u32[]{:S(2)}, u32[]{:S(2)}) collective-permute-start(f32[3,1,12,256]{3,1,2,0:T(1,128)S(1)} %constant_dynamic-update-slice_fusion), channel_id=1, source_target_pairs={{0,1},{1,2},{2,3},{3,4},{4,5},{5,6},{6,7},{7,8},{8,9},{9,10},{10,1... | collective-permute-start | bytes 110600 | tf_op jit(solution)/shard_map/ppermute | solution.py:21
  40.8 19.1 %copy-start.15 = (f32[48]{0:T(128)}, f32[48]{0:T(128)S(1)}, u32[]{:S(2)}) copy-start(f32[48]{0:T(128)S(1)} %mul.126) | copy-start | bytes 580
  42.7 15.7 %collective-permute-start.15 = (f32[3,1,12,256]{3,1,2,0:T(1,128)S(1)}, f32[3,1,12,256]{3,1,2,0:T(1,128)S(1)}, u32[]{:S(2)}, u32[]{:S(2)}) collective-permute-start(f32[3,1,12,256]{3,1,2,0:T(1,128)S(1)} %constant_dynamic-update-slice_fusion), channel_id=1, source_target_pairs={{1,0},{2,1},{3,2},{4,3},{5,4},{6,5},{7,6},{8,7},{9,8},{10,9},{11,1... | collective-permute-start | bytes 110600 | tf_op jit(solution)/shard_map/ppermute | solution.py:23
  51.2 27.9 %collective-permute-start.6 = (f32[3,1,12,4096]{3,1,2,0:T(1,128)}, f32[3,1,12,4096]{3,1,2,0:T(1,128)}, u32[]{:S(2)}, u32[]{:S(2)}) collective-permute-start(f32[3,1,12,4096]{3,1,2,0:T(1,128)} %pad_maximum_fusion.1), channel_id=1, source_target_pairs={{0,1},{1,2},{2,3},{3,4},{4,5},{5,6},{6,7},{7,8},{8,9},{9,10},{10,1... | collective-permute-start | bytes 1769480 | tf_op jit(solution)/shard_map/ppermute | solution.py:21
  53.2 27.0 %collective-permute-start.7 = (f32[3,1,12,4096]{3,1,2,0:T(1,128)}, f32[3,1,12,4096]{3,1,2,0:T(1,128)}, u32[]{:S(2)}, u32[]{:S(2)}) collective-permute-start(f32[3,1,12,4096]{3,1,2,0:T(1,128)} %pad_maximum_fusion.1), channel_id=1, source_target_pairs={{1,0},{2,1},{3,2},{4,3},{5,4},{6,5},{7,6},{8,7},{9,8},{10,9},{11,1... | collective-permute-start | bytes 1769480 | tf_op jit(solution)/shard_map/ppermute | solution.py:23
  85.5 4.0 %copy-start.7 = (s32[108,64]{1,0:T(8,128)S(1)}, s32[108,64]{1,0:T(8,128)}, u32[]{:S(2)}) copy-start(s32[108,64]{1,0:T(8,128)} %iota_add_fusion.3) | copy-start | bytes 82948
  118.4 7.7 %copy-start.16 = (f32[48]{0:T(128)S(1)}, f32[48]{0:T(128)}, u32[]{:S(2)}) copy-start(f32[48]{0:T(128)} %copy-done.15) | copy-start | bytes 580
  118.4 7.8 %copy-start.18 = (f32[48]{0:T(128)S(1)}, f32[48]{0:T(128)}, u32[]{:S(2)}) copy-start(f32[48]{0:T(128)} %reshape.345) | copy-start | bytes 580
  118.4 7.8 %copy-start.21 = (f32[48]{0:T(128)S(1)}, f32[48]{0:T(128)}, u32[]{:S(2)}) copy-start(f32[48]{0:T(128)} %compare_select_fusion.1) | copy-start | bytes 580
  119.8 6.4 %copy-start.1 = (f32[48,4096]{1,0:T(8,128)S(1)}, f32[48,4096]{1,0:T(8,128)}, u32[]{:S(2)}) copy-start(f32[48,4096]{1,0:T(8,128)} %reshape.330) | copy-start | bytes 2359300
  121.6 6.9 %copy-start.4 = (f32[48,4096]{1,0:T(8,128)S(1)}, f32[48,4096]{1,0:T(8,128)}, u32[]{:S(2)}) copy-start(f32[48,4096]{1,0:T(8,128)} %mul.125) | copy-start | bytes 2359300
  121.6 6.9 %copy-start.5 = (f32[48,4096]{1,0:T(8,128)S(1)}, f32[48,4096]{1,0:T(8,128)}, u32[]{:S(2)}) copy-start(f32[48,4096]{1,0:T(8,128)} %convolution_subtract_fusion.4) | copy-start | bytes 2359300
  121.6 6.9 %copy-start.20 = (f32[48]{0:T(128)S(1)}, f32[48]{0:T(128)}, u32[]{:S(2)}) copy-start(f32[48]{0:T(128)} %reshape.344) | copy-start | bytes 580
  121.6 10.5 %collective-permute-start.13 = (f32[2,12,256]{2,1,0:T(8,128)S(1)}, f32[2,12,256]{2,1,0:T(8,128)S(1)}, u32[]{:S(2)}, u32[]{:S(2)}) collective-permute-start(f32[2,12,256]{2,1,0:T(8,128)S(1)} %slice_bitcast_fusion.4), channel_id=1, source_target_pairs={{1,0},{2,1},{3,2},{4,3},{5,4},{6,5},{7,6},{8,7},{9,8},{10,9},{11,1... | collective-permute-start | bytes 73736 | tf_op jit(solution)/shard_map/ppermute | solution.py:33
  128.5 1.0 copy-start.19
  129.5 6.1 %copy-start.6 = (f32[108,256]{1,0:T(8,128)S(1)}, f32[108,256]{1,0:T(8,128)}, u32[]{:S(2)}) copy-start(f32[108,256]{1,0:T(8,128)} %reshape.338) | copy-start | bytes 331780
  129.5 6.1 %copy-start.9 = (f32[1,1,12,256]{3,1,2,0:T(1,128)S(1)}, f32[1,1,12,256]{3,1,2,0:T(1,128)}, u32[]{:S(2)}) copy-start(f32[1,1,12,256]{3,1,2,0:T(1,128)} %param.14) | copy-start | bytes 36868
  129.5 6.1 %copy-start.14 = (pred[12]{0:T(512)(128)(4,1)S(1)}, pred[12]{0:T(512)(128)(4,1)}, u32[]{:S(2)}) copy-start(pred[12]{0:T(512)(128)(4,1)} %get-tuple-element.23) | copy-start | bytes 40
  129.5 10.6 %copy-start.17 = (f32[48]{0:T(128)S(1)}, f32[48]{0:T(128)}, u32[]{:S(2)}) copy-start(f32[48]{0:T(128)} %reshape.342) | copy-start | bytes 580
  132.2 3.4 %collective-permute-start.14 = (f32[12,256]{1,0:T(8,128)S(1)}, f32[12,256]{1,0:T(8,128)S(1)}, u32[]{:S(2)}, u32[]{:S(2)}) collective-permute-start(f32[12,256]{1,0:T(8,128)S(1)} %slice_bitcast_fusion.6), channel_id=1, source_target_pairs={{16,0},{17,1},{18,2},{19,3},{20,4},{21,5},{22,6},{23,7},{24,8},{25... | collective-permute-start | bytes 36872 | tf_op jit(solution)/shard_map/ppermute | solution.py:33
  135.8 11.0 %collective-permute-start.16 = (f32[1,1,12,256]{3,2,1,0:T(8,128)S(1)}, f32[1,1,12,256]{3,2,1,0:T(8,128)S(1)}, u32[]{:S(2)}, u32[]{:S(2)}) collective-permute-start(f32[1,1,12,256]{3,2,1,0:T(8,128)S(1)} %bitcast.136), channel_id=1, source_target_pairs={{0,16},{1,17},{2,18},{3,19},{4,20},{5,21},{6,22},{7,23},{8,24},{9,... | collective-permute-start | bytes 36872 | tf_op jit(solution)/shard_map/ppermute | solution.py:21
  137.1 9.7 %collective-permute-start.17 = (f32[1,1,12,256]{3,2,1,0:T(8,128)S(1)}, f32[1,1,12,256]{3,2,1,0:T(8,128)S(1)}, u32[]{:S(2)}, u32[]{:S(2)}) collective-permute-start(f32[1,1,12,256]{3,2,1,0:T(8,128)S(1)} %bitcast.137), channel_id=1, source_target_pairs={{16,0},{17,1},{18,2},{19,3},{20,4},{21,5},{22,6},{23,7},{24,8},{25... | collective-permute-start | bytes 36872 | tf_op jit(solution)/shard_map/ppermute | solution.py:23
  143.8 10.1 %copy-start.3 = (pred[2,2,12,64,64]{3,4,2,1,0:T(32,128)(4,1)S(1)}, pred[2,2,12,64,64]{3,4,2,1,0:T(32,128)(4,1)}, u32[]{:S(2)}) copy-start(pred[2,2,12,64,64]{3,4,2,1,0:T(32,128)(4,1)} %add_compare_fusion.1) | copy-start | bytes 589828
  146.8 10.8 %copy-start.13 = (pred[12]{0:T(512)(128)(4,1)S(1)}, pred[12]{0:T(512)(128)(4,1)}, u32[]{:S(2)}) copy-start(pred[12]{0:T(512)(128)(4,1)} %get-tuple-element.24) | copy-start | bytes 40
  146.9 10.7 %collective-permute-start.18 = (f32[3,1,12,256]{3,2,1,0:T(8,128)S(1)}, f32[3,1,12,256]{3,2,1,0:T(8,128)S(1)}, u32[]{:S(2)}, u32[]{:S(2)}) collective-permute-start(f32[3,1,12,256]{3,2,1,0:T(8,128)S(1)} %pad_maximum_fusion.7), channel_id=1, source_target_pairs={{0,1},{1,2},{2,3},{3,4},{4,5},{5,6},{6,7},{7,8},{8,9},{9,10},{10,1... | collective-permute-start | bytes 110600 | tf_op jit(solution)/shard_map/ppermute | solution.py:21
  148.8 8.8 %collective-permute-start.19 = (f32[3,1,12,256]{3,2,1,0:T(8,128)S(1)}, f32[3,1,12,256]{3,2,1,0:T(8,128)S(1)}, u32[]{:S(2)}, u32[]{:S(2)}) collective-permute-start(f32[3,1,12,256]{3,2,1,0:T(8,128)S(1)} %pad_maximum_fusion.7), channel_id=1, source_target_pairs={{1,0},{2,1},{3,2},{4,3},{5,4},{6,5},{7,6},{8,7},{9,8},{10,9},{11,1... | collective-permute-start | bytes 110600 | tf_op jit(solution)/shard_map/ppermute | solution.py:23
  157.8 9.9 %collective-permute-start.20 = (f32[1,1,12,256]{3,2,1,0:T(8,128)S(1)}, f32[1,1,12,256]{3,2,1,0:T(8,128)S(1)}, u32[]{:S(2)}, u32[]{:S(2)}) collective-permute-start(f32[1,1,12,256]{3,2,1,0:T(8,128)S(1)} %bitcast.140), channel_id=1, source_target_pairs={{0,16},{1,17},{2,18},{3,19},{4,20},{5,21},{6,22},{7,23},{8,24},{9,... | collective-permute-start | bytes 36872 | tf_op jit(solution)/shard_map/ppermute | solution.py:21
  159.1 8.6 %collective-permute-start.21 = (f32[1,1,12,256]{3,2,1,0:T(8,128)S(1)}, f32[1,1,12,256]{3,2,1,0:T(8,128)S(1)}, u32[]{:S(2)}, u32[]{:S(2)}) collective-permute-start(f32[1,1,12,256]{3,2,1,0:T(8,128)S(1)} %bitcast.141), channel_id=1, source_target_pairs={{16,0},{17,1},{18,2},{19,3},{20,4},{21,5},{22,6},{23,7},{24,8},{25... | collective-permute-start | bytes 36872 | tf_op jit(solution)/shard_map/ppermute | solution.py:23
  165.7 11.9 %copy-start.12 = (pred[12]{0:T(512)(128)(4,1)S(1)}, pred[12]{0:T(512)(128)(4,1)}, u32[]{:S(2)}) copy-start(pred[12]{0:T(512)(128)(4,1)} %get-tuple-element.22) | copy-start | bytes 40
  167.7 28.8 %copy-start.11 = (pred[12]{0:T(512)(128)(4,1)S(1)}, pred[12]{0:T(512)(128)(4,1)}, u32[]{:S(2)}) copy-start(pred[12]{0:T(512)(128)(4,1)} %get-tuple-element.21) | copy-start | bytes 40
  167.7 9.8 %collective-permute-start.22 = (f32[3,1,12,256]{3,2,1,0:T(8,128)S(1)}, f32[3,1,12,256]{3,2,1,0:T(8,128)S(1)}, u32[]{:S(2)}, u32[]{:S(2)}) collective-permute-start(f32[3,1,12,256]{3,2,1,0:T(8,128)S(1)} %pad_maximum_fusion.8), channel_id=1, source_target_pairs={{0,1},{1,2},{2,3},{3,4},{4,5},{5,6},{6,7},{7,8},{8,9},{9,10},{10,1... | collective-permute-start | bytes 110600 | tf_op jit(solution)/shard_map/ppermute | solution.py:21
  169.6 7.9 %collective-permute-start.23 = (f32[3,1,12,256]{3,2,1,0:T(8,128)S(1)}, f32[3,1,12,256]{3,2,1,0:T(8,128)S(1)}, u32[]{:S(2)}, u32[]{:S(2)}) collective-permute-start(f32[3,1,12,256]{3,2,1,0:T(8,128)S(1)} %pad_maximum_fusion.8), channel_id=1, source_target_pairs={{1,0},{2,1},{3,2},{4,3},{5,4},{6,5},{7,6},{8,7},{9,8},{10,9},{11,1... | collective-permute-start | bytes 110600 | tf_op jit(solution)/shard_map/ppermute | solution.py:23
  175.6 15.7 %collective-permute-start.11 = (f32[2,12,4096]{2,1,0:T(8,128)}, f32[2,12,4096]{2,1,0:T(8,128)}, u32[]{:S(2)}, u32[]{:S(2)}) collective-permute-start(f32[2,12,4096]{2,1,0:T(8,128)} %slice_bitcast_fusion), channel_id=1, source_target_pairs={{1,0},{2,1},{3,2},{4,3},{5,4},{6,5},{7,6},{8,7},{9,8},{10,9},{11,1... | collective-permute-start | bytes 1179656 | tf_op jit(solution)/shard_map/ppermute | solution.py:33
  177.8 4.3 %collective-permute-start.24 = (f32[1,1,12,256]{3,2,1,0:T(8,128)S(1)}, f32[1,1,12,256]{3,2,1,0:T(8,128)S(1)}, u32[]{:S(2)}, u32[]{:S(2)}) collective-permute-start(f32[1,1,12,256]{3,2,1,0:T(8,128)S(1)} %bitcast.132), channel_id=1, source_target_pairs={{0,16},{1,17},{2,18},{3,19},{4,20},{5,21},{6,22},{7,23},{8,24},{9,... | collective-permute-start | bytes 36872 | tf_op jit(solution)/shard_map/ppermute | solution.py:21
  179.1 3.9 %collective-permute-start.25 = (f32[1,1,12,256]{3,2,1,0:T(8,128)S(1)}, f32[1,1,12,256]{3,2,1,0:T(8,128)S(1)}, u32[]{:S(2)}, u32[]{:S(2)}) collective-permute-start(f32[1,1,12,256]{3,2,1,0:T(8,128)S(1)} %bitcast.133), channel_id=1, source_target_pairs={{16,0},{17,1},{18,2},{19,3},{20,4},{21,5},{22,6},{23,7},{24,8},{25... | collective-permute-start | bytes 36872 | tf_op jit(solution)/shard_map/ppermute | solution.py:23
  183.0 13.4 %collective-permute-start.26 = (f32[3,1,12,256]{3,2,1,0:T(8,128)S(1)}, f32[3,1,12,256]{3,2,1,0:T(8,128)S(1)}, u32[]{:S(2)}, u32[]{:S(2)}) collective-permute-start(f32[3,1,12,256]{3,2,1,0:T(8,128)S(1)} %pad_maximum_fusion.9), channel_id=1, source_target_pairs={{0,1},{1,2},{2,3},{3,4},{4,5},{5,6},{6,7},{7,8},{8,9},{9,10},{10,1... | collective-permute-start | bytes 110600 | tf_op jit(solution)/shard_map/ppermute | solution.py:21
  186.3 10.1 %collective-permute-start.27 = (f32[3,1,12,256]{3,2,1,0:T(8,128)S(1)}, f32[3,1,12,256]{3,2,1,0:T(8,128)S(1)}, u32[]{:S(2)}, u32[]{:S(2)}) collective-permute-start(f32[3,1,12,256]{3,2,1,0:T(8,128)S(1)} %pad_maximum_fusion.9), channel_id=1, source_target_pairs={{1,0},{2,1},{3,2},{4,3},{5,4},{6,5},{7,6},{8,7},{9,8},{10,9},{11,1... | collective-permute-start | bytes 110600 | tf_op jit(solution)/shard_map/ppermute | solution.py:23
  192.5 0.8 copy-start.2
  193.3 4.3 %collective-permute-start.12 = (f32[12,4096]{1,0:T(8,128)S(1)}, f32[12,4096]{1,0:T(8,128)S(1)}, u32[]{:S(2)}, u32[]{:S(2)}) collective-permute-start(f32[12,4096]{1,0:T(8,128)S(1)} %slice_bitcast_fusion.2), channel_id=1, source_target_pairs={{16,0},{17,1},{18,2},{19,3},{20,4},{21,5},{22,6},{23,7},{24,8},{25... | collective-permute-start | bytes 589832 | tf_op jit(solution)/shard_map/ppermute | solution.py:33
where the time goes:
time: 201 us; the launch traced here: 199 us
  starting transfers between devices  81.1 us (40%)
  matrix products  45.5 us (23%)
  local copies, waits for them, and re-layouts  30.8 us (15%)
  waiting for transfers between devices  22.1 us (11%)
  other arithmetic  17.4 us (9%)
  between operations  2.48 us (1%)
    ppermute x12, starting transfers between devices, padded(): lax.ppermute(head, axis, [((i + 1) % count, i) for i in range(ends)])  47.1 us
    ppermute x12, starting transfers between devices, padded(): lax.ppermute(tail, axis, [(i, (i + 1) % count) for i in range(ends)])  21.9 us
    ppermute x12, waiting for transfers between devices, padded(): lax.ppermute(tail, axis, [(i, (i + 1) % count) for i in range(ends)])  17.8 us
    ppermute x4, starting transfers between devices, shifted(): lax.ppermute(value, axis, [(source, source + steps) for source in range(i...  12.1 us
    dot_general x1, matrix products, on_device(): coupling = jnp.dot(owned, flattened.T, precision=exact_mode)  8.99 us
    dot_general x4, matrix products, on_device(): coupled = jnp.dot(intersection_time, values, precision=exact_mode)  8.78 us
    dot_general x1, matrix products, on_device(): jnp.einsum('nyj,nxj->nyx', sectioned, col_pick, precision=exact_mode)  7.49 us
    dot_general x1, matrix products, on_device(): jnp.einsum('nyi,nij->nyj', row_pick, near_shapes.reshape(count_near, FP,...  6.56 us
  transfers between devices with their start and end apart: 28, of which 6 were waited for; matrix products, arithmetic and copies ran while one was open for 24% of the time, Pallas kernels for 0%

commit v1 on v0

v1 whole, which is shorter than its diff:
```python
import functools
import math

import jax
import jax.numpy as jnp
from jax import lax
from jax.experimental import pallas as pl
from jax.experimental.pallas import tpu as pltpu
from jax.sharding import PartitionSpec as P

GROUPS = 4
LANES = 128
SUBLANES = 8
TRANS_B = (((1,), (1,)), ((), ()))


def lane_iota(shape):
    return lax.broadcasted_iota(jnp.int32, shape, 1)


def sub_iota(shape):
    return lax.broadcasted_iota(jnp.int32, shape, 0)


def rolled(strips, down, right, side):
    rows = strips[0].shape[0]
    lane = lane_iota((rows, LANES))
    odd = (down % 2) == 1
    source = (lane // side) * side + (lane - right + side) % side
    source = jnp.where(odd, (source + side) % LANES, source)
    moved = [jnp.take_along_axis(strip, source, axis=1, mode="promise_in_bounds") for strip in strips]
    carry = odd & (lane < side)
    count = len(strips)
    moved = [jnp.where(carry, moved[at - 1], moved[at]) for at in range(count)]
    jump = down // 2
    bit = 1
    while bit < count:
        take = (jump // bit) % 2 == 1
        moved = [jnp.where(take, moved[(at - bit) % count], moved[at]) for at in range(count)]
        bit *= 2
    return moved


def half_swap(values):
    return pltpu.roll(values, SUBLANES // 2, axis=0)


def column_of(row, size):
    at = sub_iota((size, size)) == lane_iota((size, size))
    return jnp.sum(jnp.where(at, jnp.broadcast_to(row, (size, size)), 0), axis=1, keepdims=True)


class Sizes:
    def __init__(self, pixels, frames):
        self.pixels, self.frames = pixels, frames
        self.rest = pixels
        self.trace = pixels + pixels // 2
        self.trace_rest = self.trace + frames
        self.info = self.trace_rest + frames // 2
        self.packed = self.info + LANES


def fold_rest(rest):
    half = rest.shape[1] // 2
    full = jnp.concatenate([rest, jnp.zeros_like(rest)], axis=0)
    return jnp.where(sub_iota((SUBLANES, half)) < 4, full[:, :half], half_swap(full[:, half:]))


def pack_kernel(sizes, side, footprint_ref, anchor_ref, group_ref, count_ref, trace_ref, out_ref):
    slots = anchor_ref.shape[1]
    count = sizes.pixels // LANES
    down, right = column_of(anchor_ref[0:1, :], slots), column_of(anchor_ref[1:2, :], slots)
    group = column_of(group_ref[...], slots)
    alive = sub_iota((slots, 1)) < count_ref[0, 0]
    strips = [jnp.where(alive, footprint_ref[pl.ds(at, slots, stride=count), :], 0.0) for at in range(count)]
    strips = rolled(strips, down, right, side)
    for at, strip in enumerate(strips):
        out_ref[:, at * LANES : (at + 1) * LANES] = strip[:SUBLANES]
    for at in range(count // 2):
        pair = jnp.concatenate([strips[at][SUBLANES:], strips[at + count // 2][SUBLANES:]], axis=0)
        out_ref[:, sizes.rest + at * LANES : sizes.rest + (at + 1) * LANES] = pair
    count = sizes.frames // LANES
    strips = [trace_ref[pl.ds(at, slots, stride=count), :] for at in range(count)]
    for at, strip in enumerate(strips):
        out_ref[:, sizes.trace + at * LANES : sizes.trace + (at + 1) * LANES] = strip[:SUBLANES]
    for at in range(count // 2):
        pair = jnp.concatenate([strips[at][SUBLANES:], strips[at + count // 2][SUBLANES:]], axis=0)
        out_ref[:, sizes.trace_rest + at * LANES : sizes.trace_rest + (at + 1) * LANES] = pair
    lane = lane_iota((slots, LANES))
    info = jnp.where(lane == 0, down, jnp.where(lane == 1, right, jnp.where(lane == 2, group, alive.astype(jnp.int32))))
    info = jnp.where(lane < 4, info, 0).astype(jnp.float32)
    rest = jnp.concatenate([info[SUBLANES:], jnp.zeros((SUBLANES * 2 - slots, LANES), jnp.float32)], axis=0)
    out_ref[:, sizes.info : sizes.info + LANES] = info[:SUBLANES] + pltpu.roll(rest, 4, axis=1)


def movie_kernel(after_ref, movie_ref, out_ref, sem):
    copy = pltpu.make_async_copy(movie_ref, out_ref, sem)
    copy.start()
    copy.wait()


def gather_rows(tops, rests):
    rows = list(tops)
    low = sub_iota(rests[0].shape) < 4
    for one, two in ((0, 1), (2, 3)):
        first = jnp.where(low, rests[one], half_swap(rests[two]))
        second = jnp.where(low, half_swap(rests[one]), rests[two])
        rows.append(jnp.concatenate([first, second], axis=1))
    return jnp.concatenate(rows, axis=0)


def tile_labels(sizes, tiles):
    infos = [tile[:, sizes.info :] for tile in tiles]
    turned = [pltpu.roll(info, LANES - 4, axis=1) for info in infos]
    low = sub_iota((SUBLANES, LANES)) < 4
    labels = jnp.concatenate(
        infos
        + [jnp.where(low, turned[0], half_swap(turned[1])), jnp.where(low, turned[2], half_swap(turned[3]))],
        axis=0,
    )
    down, right = labels[:, 0:1].astype(jnp.int32), labels[:, 1:2].astype(jnp.int32)
    group = jnp.where(labels[:, 3:4] > 0, labels[:, 2:3].astype(jnp.int32), -1)
    row = sub_iota(group.shape)
    block = jnp.where(row < 32, row // 8, (row - 32) // 4)
    return down, right, group, block >= 2, (block % 2) == 1


def tile_traces(sizes, tiles):
    return gather_rows(
        [tile[:, sizes.trace : sizes.trace + sizes.frames] for tile in tiles],
        [tile[:, sizes.trace_rest : sizes.trace_rest + sizes.frames // 2] for tile in tiles],
    )


def share_kernel(
    sizes, side, devices, own_ref, west_ref, north_ref, corner_ref, movie_ref, back_ref, back_trace_ref,
    value_ref, code_ref, split_ref, *outs,
):
    tiles = (own_ref, west_ref, north_ref, corner_ref)
    count = split_ref.shape[0] // 2 - 8
    pixels, frames = sizes.pixels, sizes.frames
    part = 512
    down, right, group, from_north, from_west = tile_labels(sizes, tiles)
    lane = lane_iota((count, part))
    for at in range(0, pixels, part):
        half = pixels // 2
        tops = [tile[:, at : at + part] for tile in tiles]
        where_rest = sizes.rest + at % half
        rests = [tile[:, where_rest : where_rest + part] for tile in tiles]
        sub_low = sub_iota((SUBLANES, part)) < 4
        pairs = []
        for one, two in ((0, 1), (2, 3)):
            if at < half:
                pairs.append(jnp.where(sub_low, rests[one], half_swap(rests[two])))
            else:
                pairs.append(jnp.where(sub_low, half_swap(rests[one]), rests[two]))
        raw = jnp.concatenate(tops + pairs, axis=0)
        spot = lane + at
        above, before = (spot // side) < down, (spot % side) < right
        covered = (above == from_north) & (before == from_west)
        value = jnp.where(covered, raw, 0.0)
        value_ref[:, at : at + part] = value
        code_ref[:, at : at + part] = jnp.where(covered, group, -1)
        high = value.astype(jnp.bfloat16)
        split_ref[0:count, at : at + part] = high
        split_ref[count : 2 * count, at : at + part] = (value - high.astype(jnp.float32)).astype(jnp.bfloat16)
    split_ref[2 * count : 2 * count + 16, :] = back_ref[...]
    share = jnp.dot(split_ref[0:count, :], movie_ref[...], preferred_element_type=jnp.float32)
    product = lax.dot_general(
        split_ref[0 : 2 * count, :], split_ref[...], TRANS_B, preferred_element_type=jnp.float32
    )
    product = product[:count] + product[count:]
    gram = product[:, :count] + product[:, count : 2 * count]
    for at in range(2):
        share = share - product[:, 2 * count + at : 2 * count + at + 1] * back_trace_ref[at : at + 1, :]
    wide = jnp.concatenate([gram, jnp.zeros((count, LANES - count), jnp.float32)], axis=1)
    if len(outs) > 2:
        share_out, gram_out, _ = outs
        share_out[...] = share
        gram_out[...] = wide
        return
    send_ref, turned_ref = outs
    traces = tile_traces(sizes, tiles)
    own_rows = lambda values: [values[0:8], values[32:40]]
    table = jnp.concatenate(
        [share] + own_rows(traces) + own_rows(jnp.broadcast_to(group.astype(jnp.float32), (count, frames)))
        + [jnp.zeros((LANES - count - 32, frames), jnp.float32)],
        axis=0,
    )
    turned_ref[...] = jnp.transpose(table)
    chunk = [wide[8 * at : 8 * at + 8] for at in range(6)]
    place = lane_iota((8, LANES))
    first = pltpu.roll(chunk[0], 80, axis=1)
    tail = pltpu.roll(chunk[5], 96, axis=1)
    second = chunk[1] + pltpu.roll(chunk[2], 48, axis=1) + jnp.where(place >= 96, tail, 0.0)
    third = chunk[3] + pltpu.roll(chunk[4], 48, axis=1) + pltpu.roll(jnp.where(place < 16, tail, 0.0), 96, axis=1)
    for at in range(devices):
        send_ref[at, 0:8, :] = turned_ref[pl.ds(at, 8, stride=devices), :] + first
        send_ref[at, 8:16, :] = second
        send_ref[at, 16:24, :] = third


def shape_kernel(
    sizes, own_ref, west_ref, north_ref, corner_ref, movie_ref, back_ref, back_trace_ref, window_ref,
    start_ref, code_ref, parts_ref, own_out, west_out, row_out, value_ref, goal_ref, split_ref,
):
    tiles = (own_ref, west_ref, north_ref, corner_ref)
    count = value_ref.shape[0]
    pixels, frames = sizes.pixels, sizes.frames
    part = 512
    group = tile_labels(sizes, tiles)[2]
    traces = tile_traces(sizes, tiles)
    moment = lane_iota((count, frames))
    inside = (moment >= window_ref[0]) & (moment < window_ref[1])
    weighted = jnp.where(inside, traces, 0.0)
    overlap = lax.dot_general(
        weighted, weighted, TRANS_B, precision=lax.Precision.HIGHEST, preferred_element_type=jnp.float32
    )
    mass = jnp.sum(weighted * weighted, axis=1, keepdims=True)
    inverse = 1.0 / jnp.where(group >= 0, mass, 1.0)
    overlap = jnp.where(sub_iota((count, count)) == lane_iota((count, count)), 0.0, overlap * inverse)
    rate = jnp.concatenate([overlap, overlap], axis=1)
    rate_high = rate.astype(jnp.bfloat16)
    rate_low = (rate - rate_high.astype(jnp.float32)).astype(jnp.bfloat16)
    rates = jnp.concatenate([rate_high, rate_low], axis=0)
    loads = [
        jnp.sum(weighted * back_trace_ref[at : at + 1, :], axis=1, keepdims=True) * inverse for at in range(2)
    ]
    rounded = weighted.astype(jnp.bfloat16)
    for at in range(0, pixels, part):
        goal = lax.dot_general(
            rounded, movie_ref[at : at + part, :], TRANS_B, preferred_element_type=jnp.float32
        ) * inverse
        for back in range(2):
            goal = goal - loads[back] * back_ref[back : back + 1, at : at + part].astype(jnp.float32)
        goal_ref[:, at : at + part] = goal
    for step in range(GROUPS):
        values, parts = (start_ref, parts_ref) if step == 0 else (value_ref, split_ref)
        for at in range(0, pixels, part):
            coupled = jnp.dot(rates, parts[0 : 2 * count, at : at + part], preferred_element_type=jnp.float32)
            coupled = coupled[:count] + coupled[count:]
            value = jnp.where(
                code_ref[:, at : at + part] == step,
                jnp.maximum(goal_ref[:, at : at + part] - coupled, 0.0),
                values[:, at : at + part],
            )
            value_ref[:, at : at + part] = value
            if step < GROUPS - 1:
                high = value.astype(jnp.bfloat16)
                split_ref[0:count, at : at + part] = high
                split_ref[count : 2 * count, at : at + part] = (value - high.astype(jnp.float32)).astype(jnp.bfloat16)
    half = pixels // 2
    own_out[:, :pixels] = value_ref[0:8, :]
    west_out[:, :pixels] = value_ref[8:16, :]
    row_out[0:8, :pixels] = value_ref[16:24, :]
    row_out[8:16, :pixels] = value_ref[24:32, :]
    low = sub_iota((SUBLANES, half)) < 4
    for base, even, odd, shift in ((32, own_out, west_out, 0), (40, row_out, row_out, 8)):
        left, right_half = value_ref[base : base + 8, :half], value_ref[base : base + 8, half:]
        even[0:8, pixels:] = jnp.where(low, left, half_swap(right_half))
        odd[shift : shift + 8, pixels:] = jnp.where(low, half_swap(left), right_half)


def trace_kernel(rows, cols, step_frames, recv_ref, out_ref, coupling_ref, near_ref, turned_ref):
    count = 4 * 12
    lane = lane_iota((SUBLANES * 6, LANES))
    west = LANES - step_frames
    low = sub_iota((SUBLANES, LANES)) < 4
    shares, starts, codes, selfs = [], [], [], []
    for r in range(rows):
        tables = [
            jnp.transpose(recv_ref[r * cols : (r + 1) * cols, 8 * at : 8 * at + 8, :].reshape(LANES, LANES))
            for at in range(3)
        ]
        shares.append(tables[0][0:48])
        starts.append((tables[0][48:56], tables[0][56:64]))
        codes.append((tables[0][64:72], tables[0][72:80]))
        chunks = [
            tables[0][80:128], tables[1][0:48], tables[1][48:96], tables[2][0:48], tables[2][48:96],
            jnp.concatenate([tables[1][96:128], tables[2][96:112]], axis=0),
        ]
        pieces = []
        for a, chunk in enumerate(chunks):
            diagonal = jnp.zeros((SUBLANES, LANES), jnp.float32)
            for t in range(SUBLANES):
                spread = jnp.take_along_axis(
                    chunk, (lane // SUBLANES) * SUBLANES + t, axis=1, mode="promise_in_bounds"
                )
                here = sub_iota((SUBLANES, LANES)) == t
                same = spread[8 * a : 8 * a + 8]
                diagonal = diagonal + jnp.where(here, same, 0.0)
                coupling_ref[r, 8 * a + t] = spread
                coupling_ref[r, 8 * a + t, 8 * a : 8 * a + 8] = jnp.where(here, 0.0, same)
            pieces.append(diagonal)
        selfs.append(jnp.concatenate(pieces, axis=0))

    def collect(per_tile, r):
        here = per_tile[r]
        top = here[0:8] + pltpu.roll(here[8:16], west, axis=1)
        rest = here[32:40] + half_swap(pltpu.roll(here[32:40], west, axis=1))
        if r + 1 < rows:
            below = per_tile[r + 1]
            top = top + below[16:24] + pltpu.roll(below[24:32], west, axis=1)
            rest = rest + below[40:48] + half_swap(pltpu.roll(below[40:48], west, axis=1))
        return top, rest

    drive = [collect(shares, r) for r in range(rows)]
    weight = [collect(selfs, r) for r in range(rows)]
    inverse = [
        [1.0 / jnp.where(code >= 0, total, 1.0) for code, total in zip(codes[r], weight[r])] for r in range(rows)
    ]
    current = [list(starts[r]) for r in range(rows)]
    for step in range(GROUPS):
        for r in range(rows):
            top, rest = current[r]
            rest_pair = jnp.where(low, rest, half_swap(pltpu.roll(rest, step_frames, axis=1)))
            near_ref[r, 0:8] = top
            near_ref[r, 8:16] = pltpu.roll(top, step_frames, axis=1)
            near_ref[r, 32:40] = rest_pair
            if r + 1 < rows:
                near_ref[r + 1, 16:24] = top
                near_ref[r + 1, 24:32] = pltpu.roll(top, step_frames, axis=1)
                near_ref[r + 1, 40:48] = rest_pair
            if r == 0:
                near_ref[r, 16:32] = jnp.zeros((16, LANES), jnp.float32)
                near_ref[r, 40:48] = jnp.zeros((8, LANES), jnp.float32)
        sums = []
        for r in range(rows):
            total = jnp.zeros((count, LANES), jnp.float32)
            for k in range(count):
                total = total + coupling_ref[r, k] * near_ref[r, k : k + 1, :]
            sums.append(total)
        for r in range(rows):
            for at, coupled in enumerate(collect(sums, r)):
                updated = jnp.maximum((drive[r][at] - coupled) * inverse[r][at], 0.0)
                current[r][at] = jnp.where(codes[r][at] == step, updated, current[r][at])
    for r in range(rows):
        table = jnp.concatenate(
            [current[r][0], jnp.where(low, current[r][1], 0.0), jnp.zeros((LANES - 16, LANES), jnp.float32)], axis=0
        )
        turned_ref[...] = jnp.transpose(table)
        out = jnp.zeros((cols, LANES), jnp.float32)
        for t in range(step_frames):
            out = out + pltpu.roll(turned_ref[pl.ds(t, cols, stride=step_frames), :], 16 * t, axis=1)
        out_ref[r * cols : (r + 1) * cols, :] = out


def finish_kernel(sizes, side, slices, own_ref, row_ref, east_ref, anchor_ref, *refs):
    slots = anchor_ref.shape[1]
    pixels, half = sizes.pixels, sizes.pixels // 2
    count = pixels // LANES
    new_footprint_ref = refs[-2] if slices else refs[-1]
    back_down = (side - column_of(anchor_ref[0:1, :], slots)) % side
    back_right = (side - column_of(anchor_ref[1:2, :], slots)) % side
    strips = []
    for at in range(0, pixels, LANES):
        where_rest = pixels + at % half
        top = own_ref[:, at : at + LANES] + row_ref[0:8, at : at + LANES] + east_ref[:, at : at + LANES]
        rest = (
            own_ref[:, where_rest : where_rest + LANES]
            + row_ref[0:8, where_rest : where_rest + LANES]
            + east_ref[:, where_rest : where_rest + LANES]
        )
        if at >= half:
            rest = half_swap(rest)
        strips.append(jnp.concatenate([top, rest[: slots - SUBLANES]], axis=0))
    strips = rolled(strips, back_down, back_right, side)
    for at, strip in enumerate(strips):
        new_footprint_ref[pl.ds(at, slots, stride=count), :] = strip
    if not slices:
        return
    recv_ref, _, new_trace_ref = refs
    table = jnp.transpose(
        jnp.concatenate([recv_ref[...], jnp.zeros((LANES - slices, LANES), jnp.float32)], axis=0)
    )
    per = LANES // slices
    count = sizes.frames // LANES
    for tile in range(count):
        out = jnp.zeros((16, LANES), jnp.float32)
        for at in range(per):
            t = tile * per + at
            out = out + pltpu.roll(table[16 * t : 16 * t + 16], slices * at, axis=1)
        new_trace_ref[pl.ds(tile, slots, stride=count), :] = out[:slots]


def padded(cells, sides):
    for axis, dim in sides:
        size = cells.shape[dim]
        head = lax.slice_in_dim(cells, 0, 1, axis=dim)
        tail = lax.slice_in_dim(cells, size - 1, size, axis=dim)
        cells = jnp.concatenate([shifted(tail, axis, 1), cells, shifted(head, axis, -1)], axis=dim)
    return cells


def relax_by_neighbours(share, gram, traces, group, alive):
    slots, frames = traces.shape
    rows_of = lambda values: [
        jnp.concatenate([values[8 * b : 8 * b + 8], values[32 + 4 * b : 36 + 4 * b]], axis=0) for b in range(4)
    ]
    shares = rows_of(share)
    grams = [rows_of(part.T) for part in rows_of(gram)]
    near = []
    for b in range(4):
        cells = [[jnp.zeros((slots, slots), jnp.float32)] * 3 for _ in range(3)]
        for k in range(4):
            cells[1 + b // 2 - k // 2][1 + b % 2 - k % 2] = grams[b][k].T
        near.append(jnp.concatenate([cell for row in cells for cell in row], axis=1))
    both = jnp.stack([jnp.concatenate(pair, axis=1) for pair in zip(shares, near)]).reshape(2, 2, slots, -1)
    column_sum = both[:, 0] + shifted(both[:, 1], "col", -1)
    total = column_sum[0] + shifted(column_sum[1], "row", -1)
    drives, coupling = total[:, :frames], total[:, frames:]
    weight = jnp.diagonal(coupling[:, 4 * slots : 5 * slots])
    weight = jnp.where(alive, weight, 1.0)
    for step in range(GROUPS):
        nearby = padded(traces[None, None], (("row", 0), ("col", 1))).reshape(9 * slots, frames)
        coupled = jnp.dot(coupling, nearby, precision=lax.Precision.HIGHEST)
        updated = jnp.maximum(traces + (drives - coupled) / weight[:, None], 0.0)
        traces = jnp.where((alive & (group == step))[:, None], updated, traces)
    return traces


def shifted(value, axis, steps):
    count = lax.axis_size(axis)
    initial, last = (max(0, -steps), min(count, count - steps))
    return lax.ppermute(value, axis, [(source, source + steps) for source in range(initial, last)])


VMEM = pl.BlockSpec(memory_space=pltpu.VMEM)
SMEM = pl.BlockSpec(memory_space=pltpu.SMEM)


def kernel_params(megabytes):
    return pltpu.CompilerParams(vmem_limit_bytes=megabytes * 2**20)


def on_device(rows, cols, movie, footprints, anchors, groups, counts, temporal, back_spatial, back_temporal, window):
    tile_rows, tile_cols, frames = movie.shape
    slots = footprints.shape[2]
    pixels = tile_rows * tile_cols
    side = tile_cols
    assert pixels == footprints.shape[3] and tile_rows == side and 2 * side == LANES and slots == 12
    devices = rows * cols
    step_frames = frames // devices
    sliced = step_frames * devices == frames and step_frames == SUBLANES and cols * step_frames == LANES
    count = 4 * slots
    sizes = Sizes(pixels, frames)
    anchor = anchors[0, 0].T
    f32 = lambda *shape: jax.ShapeDtypeStruct(shape, jnp.float32)
    packed = pl.pallas_call(
        functools.partial(pack_kernel, sizes, side),
        out_shape=f32(SUBLANES, sizes.packed),
        in_specs=[VMEM, VMEM, VMEM, SMEM, VMEM],
        out_specs=VMEM,
        compiler_params=kernel_params(3),
        name="pack",
    )(footprints.reshape(-1, LANES), anchor, groups[0], counts, temporal.reshape(-1, LANES))
    north = shifted(packed, "row", 1)
    west = shifted(packed, "col", 1)
    corner = shifted(west, "row", 1)
    near_movie = pl.pallas_call(
        movie_kernel,
        out_shape=jax.ShapeDtypeStruct((pixels, frames), movie.dtype),
        in_specs=[pl.BlockSpec(memory_space=pl.ANY)] * 2,
        out_specs=VMEM,
        scratch_shapes=[pltpu.SemaphoreType.DMA(())],
        compiler_params=kernel_params(3),
        cost_estimate=pl.CostEstimate(flops=10**7, bytes_accessed=pixels * frames * 4, transcendentals=0),
        name="stage",
    )(packed, movie.reshape(pixels, frames))
    back = jnp.pad(back_spatial.reshape(2, pixels), ((0, 14), (0, 0)))
    if sliced:
        share_outs, share_scratch = (f32(devices, 24, LANES),), [pltpu.VMEM((frames, LANES), jnp.float32)]
    else:
        share_outs = (f32(count, frames), f32(count, LANES))
        share_scratch = [pltpu.VMEM((SUBLANES, LANES), jnp.float32)]
    canvas, code, split, *shares = pl.pallas_call(
        functools.partial(share_kernel, sizes, side, devices),
        out_shape=(
            f32(count, pixels),
            jax.ShapeDtypeStruct((count, pixels), jnp.int32),
            jax.ShapeDtypeStruct((2 * count + 16, pixels), jnp.bfloat16),
        )
        + share_outs,
        in_specs=[VMEM] * 7,
        out_specs=(VMEM,) * (3 + len(share_outs)),
        scratch_shapes=share_scratch,
        compiler_params=kernel_params(10),
        cost_estimate=pl.CostEstimate(flops=10**9, bytes_accessed=8 * 2**20, transcendentals=0),
        name="share",
    )(packed, west, north, corner, near_movie, back, back_temporal)
    own_part, west_part, row_part = pl.pallas_call(
        functools.partial(shape_kernel, sizes),
        out_shape=(f32(SUBLANES, sizes.trace), f32(SUBLANES, sizes.trace), f32(2 * SUBLANES, sizes.trace)),
        in_specs=[VMEM] * 7 + [SMEM] + [VMEM] * 3,
        out_specs=(VMEM,) * 3,
        scratch_shapes=[
            pltpu.VMEM((count, pixels), jnp.float32),
            pltpu.VMEM((count, pixels), jnp.float32),
            pltpu.VMEM((2 * count, pixels), jnp.bfloat16),
        ],
        compiler_params=kernel_params(12),
        cost_estimate=pl.CostEstimate(flops=10**9, bytes_accessed=8 * 2**20, transcendentals=0),
        name="shape",
    )(packed, west, north, corner, near_movie, back, back_temporal, window, canvas, code, split)
    from_south = shifted(row_part, "row", -1)
    from_east = shifted(west_part + from_south[SUBLANES:], "col", -1)
    if sliced:
        received = lax.all_to_all(shares[0], ("row", "col"), 0, 0, tiled=True)
        relaxed = pl.pallas_call(
            functools.partial(trace_kernel, rows, cols, step_frames),
            out_shape=f32(devices, LANES),
            in_specs=[VMEM],
            out_specs=VMEM,
            scratch_shapes=[
                pltpu.VMEM((rows, count, count, LANES), jnp.float32),
                pltpu.VMEM((rows, count, LANES), jnp.float32),
                pltpu.VMEM((LANES, LANES), jnp.float32),
            ],
            compiler_params=kernel_params(6),
            cost_estimate=pl.CostEstimate(flops=10**9, bytes_accessed=2**20, transcendentals=0),
            name="relax",
        )(received)
        extra = (lax.all_to_all(relaxed, ("row", "col"), 0, 0, tiled=True),)
    else:
        alive = jnp.arange(slots, dtype=jnp.int32) < counts[0, 0]
        traces = relax_by_neighbours(shares[0], shares[1][:, :count], temporal[0, 0], groups[0, 0], alive)
        extra = ()
    new_footprints, *new_traces = pl.pallas_call(
        functools.partial(finish_kernel, sizes, side, devices if sliced else 0),
        out_shape=(f32(slots * pixels // LANES, LANES),) + (f32(slots * frames // LANES, LANES),) * len(extra),
        in_specs=[VMEM] * (4 + len(extra)),
        out_specs=(VMEM,) * (1 + len(extra)),
        compiler_params=kernel_params(4),
        name="finish",
    )(own_part, from_south, from_east, anchor, *extra)
    if sliced:
        traces = new_traces[0]
    return new_footprints.reshape(footprints.shape), traces.reshape(temporal.shape)


def solution(mesh):
    return jax.shard_map(
        functools.partial(on_device, mesh.shape["row"], mesh.shape["col"]),
        mesh=mesh,
        in_specs=(
            P("row", "col", None),
            P("row", "col", None, None),
            P("row", "col", None, None),
            P("row", "col", None),
            P("row", "col"),
            P("row", "col", None, None),
            P(None, "row", "col"),
            P(),
            P(),
        ),
        out_specs=(P("row", "col", None, None), P("row", "col", None, None)),
        check_vma=False,
    )
```

time: 201 us -> 59.7 us (0.30)
  the two profiles are of different devices: /device:TPU:17 before, /device:TPU:0 now
where the time goes in v1:
time: 59.7 us; the launch traced here: 59.1 us
  waiting for transfers between devices  22.7 us (38%)
  starting transfers between devices  20.4 us (34%)
  Pallas kernels  8.66 us (15%)
  local copies, waits for them, and re-layouts  5.92 us (10%)
  between operations  1.44 us (2%)
    all_to_all x1, waiting for transfers between devices, on_device(): received = lax.all_to_all(shares[0], ('row', 'col'), 0, 0, tiled=True)  12.6 us
    ppermute x5, starting transfers between devices, shifted(): lax.ppermute(value, axis, [(source, source + steps) for source in range(i...  10.2 us
    all_to_all x1, starting transfers between devices, on_device(): received = lax.all_to_all(shares[0], ('row', 'col'), 0, 0, tiled=True)  7.6 us
    all_to_all x1, waiting for transfers between devices, on_device(): extra = (lax.all_to_all(relaxed, ('row', 'col'), 0, 0, tiled=True),)  7.07 us
    unnamed x16, local copies, waits for them, and re-layouts  5.05 us
    ppermute x5, waiting for transfers between devices, shifted(): lax.ppermute(value, axis, [(source, source + steps) for source in range(i...  3.01 us
    pallas_call x1, Pallas kernels, on_device(): pl.pallas_call(functools.partial(trace_kernel, rows, cols, step_frames),...  2.64 us
    all_to_all x1, starting transfers between devices, on_device(): extra = (lax.all_to_all(relaxed, ('row', 'col'), 0, 0, tiled=True),)  2.54 us
  transfers between devices with their start and end apart: 7, of which 3 were waited for; matrix products, arithmetic and copies ran while one was open for 2% of the time, Pallas kernels for 5%

profile of v1, /device:TPU:0, one launch (start us, length us, event | category | flops | bytes accessed | tf_op | source)
XLA Modules:
  0.0 59.1 jit_solution(18009141589654988396)
XLA Ops:
  1.3 0.0 copy-start.1
  1.3 0.9 %copy-done.1 = f32[1,1,12,4096]{3,1,2,0:T(1,128)S(1)} copy-done((f32[1,1,12,4096]{3,1,2,0:T(1,128)S(1)}, f32[1,1,12,4096]{3,1,2,0:T(1,128)}, u32[]{:S(2)}) %copy-start.1) | copy-done | bytes 196632
  2.2 0.0 copy-start.2
  2.2 0.7 %copy-done.2 = f32[1,1,12,256]{3,1,2,0:T(1,128)S(1)} copy-done((f32[1,1,12,256]{3,1,2,0:T(1,128)S(1)}, f32[1,1,12,256]{3,1,2,0:T(1,128)}, u32[]{:S(2)}) %copy-start.2) | copy-done | bytes 12312
  2.9 0.0 copy-start.3
  2.9 0.7 %copy-done.3 = s32[1,1,12,2]{2,3,1,0:T(2,128)S(1)} copy-done((s32[1,1,12,2]{2,3,1,0:T(2,128)S(1)}, s32[1,1,12,2]{2,3,1,0:T(2,128)}, u32[]{:S(2)}) %copy-start.3) | copy-done | bytes 120
  3.6 0.0 copy-start.6
  3.6 0.7 %copy-done.6 = s32[1,1,12]{2,1,0:T(1,128)S(1)} copy-done((s32[1,1,12]{2,1,0:T(1,128)S(1)}, s32[1,1,12]{2,1,0:T(1,128)}, u32[]{:S(2)}) %copy-start.6) | copy-done | bytes 72
  4.2 0.3 pack.1.after_ref.own_ref
  4.6 4.9 %collective-permute-start = (f32[8,6656]{1,0:T(8,128)S(1)}, f32[8,6656]{1,0:T(8,128)S(1)}, u32[]{:S(2)}, u32[]{:S(2)}) collective-permute-start(f32[8,6656]{1,0:T(8,128)S(1)} %pack.1.after_ref.own_ref), channel_id=1, source_target_pairs={{0,1},{1,2},{2,3},{3,4},{4,5},{5,6},{6,7},{7,8},{8,9},{9,10},{10,1... | collective-permute-start | bytes 638984 | tf_op jit(solution)/shard_map/ppermute | solution.py:425
  9.5 1.5 %collective-permute-start.1 = (f32[8,6656]{1,0:T(8,128)S(1)}, f32[8,6656]{1,0:T(8,128)S(1)}, u32[]{:S(2)}, u32[]{:S(2)}) collective-permute-start(f32[8,6656]{1,0:T(8,128)S(1)} %pack.1.after_ref.own_ref), channel_id=1, source_target_pairs={{0,16},{1,17},{2,18},{3,19},{4,20},{5,21},{6,22},{7,23},{8,24},{9,... | collective-permute-start | bytes 638984 | tf_op jit(solution)/shard_map/ppermute | solution.py:425
  10.9 3.0 %collective-permute-done.west_ref = f32[8,6656]{1,0:T(8,128)S(1)} collective-permute-done((f32[8,6656]{1,0:T(8,128)S(1)}, f32[8,6656]{1,0:T(8,128)S(1)}, u32[]{:S(2)}, u32[]{:S(2)}) %collective-permute-start) | collective-permute-done | bytes 213024 | tf_op jit(solution)/shard_map/ppermute | solution.py:425
  13.9 1.3 %collective-permute-start.2 = (f32[8,6656]{1,0:T(8,128)S(1)}, f32[8,6656]{1,0:T(8,128)S(1)}, u32[]{:S(2)}, u32[]{:S(2)}) collective-permute-start(f32[8,6656]{1,0:T(8,128)S(1)} %collective-permute-done.west_ref), channel_id=1, source_target_pairs={{0,16},{1,17},{2,18},{3,19},{4,20},{5,21},{6,22},{7,23},{8,24},{9,... | collective-permute-start | bytes 638984 | tf_op jit(solution)/shard_map/ppermute | solution.py:425
  15.2 0.9 %reshape.27 = bf16[2,4096]{1,0:T(2,128)(2,1)S(1)} reshape(bf16[2,64,64]{2,1,0:T(8,128)(2,1)} %param.15) | data formatting | bytes 32768 | tf_op jit(solution)/shard_map/reshape | solution.py:470
  16.1 0.0 copy-start
  16.1 1.6 %copy-done = bf16[64,64,256]{2,1,0:T(8,128)(2,1)S(1)} copy-done((bf16[64,64,256]{2,1,0:T(8,128)(2,1)S(1)}, bf16[64,64,256]{2,1,0:T(8,128)(2,1)}, u32[]{:S(2)}) %copy-start) | copy-done | bytes 2097176
  17.7 0.0 copy-start.5
  17.7 0.1 stage.1.movie_ref
  17.9 0.0 copy-start.7
  17.9 0.0 collective-permute-done.1.north_ref
  17.9 0.0 collective-permute-done.2.corner_ref
  17.9 0.5 copy-done.5
  18.4 2.1 %share.1 = (f32[48,4096]{1,0:T(8,128)S(1)}, s32[48,4096]{1,0:T(8,128)S(1)}, bf16[112,4096]{1,0:T(8,128)(2,1)S(1)}, f32[32,24,128]{2,1,0:T(8,128)}) custom-call(f32[8,6656]{1,0:T(8,128)S(1)} %pack.1.after_ref.own_ref, f32[8,6656]{1,0:T(8,128)S(1)} %collective-permute-done.west_ref, f32[8,6656]{1,0:T(8,128)S(1)} %collective-permute-done.1.north_ref, ...), custom_call_target="tpu_custom_call" | custom-call | flops 1000000000 | bytes 8388608 | tf_op jit(solution)/shard_map/share/pallas_call | solution.py:476
  20.5 0.0 copy-done.7
  20.5 2.4 %shape.1 = (f32[8,6144]{1,0:T(8,128)S(1)}, f32[8,6144]{1,0:T(8,128)S(1)}, f32[16,6144]{1,0:T(8,128)S(1)}) custom-call(f32[8,6656]{1,0:T(8,128)S(1)} %pack.1.after_ref.own_ref, f32[8,6656]{1,0:T(8,128)S(1)} %collective-permute-done.west_ref, f32[8,6656]{1,0:T(8,128)S(1)} %collective-permute-done.1.north_ref, f32[8,6656]{1,0:T(8,128)S(1)} %collective-permute-done.2.corner_ref, ...), custom_call_target="tpu_custom_call" | custom-call | flops 1000000000 | bytes 8388608 | tf_op jit(solution)/shard_map/shape/pallas_call | solution.py:491
  22.9 1.3 %collective-permute-start.3 = (f32[16,6144]{1,0:T(8,128)S(1)}, f32[16,6144]{1,0:T(8,128)S(1)}, u32[]{:S(2)}, u32[]{:S(2)}) collective-permute-start(f32[16,6144]{1,0:T(8,128)S(1)} %get-tuple-element.15), channel_id=1, source_target_pairs={{16,0},{17,1},{18,2},{19,3},{20,4},{21,5},{22,6},{23,7},{24,8},{25... | collective-permute-start | bytes 1179656 | tf_op jit(solution)/shard_map/ppermute | solution.py:425
  24.2 7.6 %all-to-all-start = ((f32[32,24,128]{2,1,0:T(8,128)}), f32[32,24,128]{2,1,0:T(8,128)S(1)}, u32[]{:S(2)}, u32[]{:S(2)}) async-start(f32[32,24,128]{2,1,0:T(8,128)} %get-tuple-element.17), calls=%async_computation | async-start | bytes 786432 | tf_op jit(solution)/shard_map/all_to_all | solution.py:508
  31.8 0.0 collective-permute-done.3.row_ref
  31.8 0.0 copy-start.4
  31.8 1.3 %collective-permute-start.4 = (f32[8,6144]{1,0:T(8,128)S(1)}, f32[8,6144]{1,0:T(8,128)S(1)}, u32[]{:S(2)}, u32[]{:S(2)}) collective-permute-start(f32[8,6144]{1,0:T(8,128)S(1)} %slice_add_fusion), channel_id=1, source_target_pairs={{1,0},{2,1},{3,2},{4,3},{5,4},{6,5},{7,6},{8,7},{9,8},{10,9},{11,1... | collective-permute-start | bytes 589832 | tf_op jit(solution)/shard_map/ppermute | solution.py:425
  33.1 12.6 %all-to-all-done.recv_ref = f32[32,24,128]{2,1,0:T(8,128)S(1)} async-done(((f32[32,24,128]{2,1,0:T(8,128)}), f32[32,24,128]{2,1,0:T(8,128)S(1)}, u32[]{:S(2)}, u32[]{:S(2)}) %all-to-all-start) | async-done | bytes 393248 | tf_op jit(solution)/shard_map/all_to_all | solution.py:508
  45.8 2.6 %relax.1 = f32[32,128]{1,0:T(8,128)} custom-call(f32[32,24,128]{2,1,0:T(8,128)S(1)} %all-to-all-done.recv_ref), custom_call_target="tpu_custom_call" | custom-call | flops 1000000000 | bytes 1048576 | tf_op jit(solution)/shard_map/relax/pallas_call | solution.py:509
  48.4 2.5 %all-to-all-start.1 = ((f32[32,1,128]{2,1,0:T(1,128)}), f32[32,1,128]{2,1,0:T(1,128)S(1)}, u32[]{:S(2)}, u32[]{:S(2)}) async-start(f32[32,1,128]{2,1,0:T(1,128)} %bitcast.7), calls=%async_computation.1 | async-start | bytes 32768 | tf_op jit(solution)/shard_map/all_to_all | solution.py:523
  51.0 0.0 collective-permute-done.4.east_ref
  51.0 7.1 %all-to-all-done.1 = f32[32,1,128]{2,1,0:T(1,128)S(1)} async-done(((f32[32,1,128]{2,1,0:T(1,128)}), f32[32,1,128]{2,1,0:T(1,128)S(1)}, u32[]{:S(2)}, u32[]{:S(2)}) %all-to-all-start.1) | async-done | bytes 16416 | tf_op jit(solution)/shard_map/all_to_all | solution.py:523
  58.0 0.0 copy-done.4
  58.0 1.1 %finish.1 = (f32[384,128]{1,0:T(8,128)}, f32[24,128]{1,0:T(8,128)}) custom-call(f32[8,6144]{1,0:T(8,128)S(1)} %get-tuple-element.14.own_ref, f32[16,6144]{1,0:T(8,128)S(1)} %collective-permute-done.3.row_ref, f32[8,6144]{1,0:T(8,128)S(1)} %collective-permute-done.4.east_ref, s32[2,12]{1,0:T(2,128)S(1)} %bitcast.18, f32[32,128]{1,0:T(8,128)S(1)} %bitcast.15), custom_call_target="tpu_custom_call" | custom-call | tf_op jit(solution)/shard_map/finish/pallas_call | solution.py:528
  (2 shorter events, 0.0 us)
Async XLA Ops:
  1.3 0.9 %copy-start.1 = (f32[1,1,12,4096]{3,1,2,0:T(1,128)S(1)}, f32[1,1,12,4096]{3,1,2,0:T(1,128)}, u32[]{:S(2)}) copy-start(f32[1,1,12,4096]{3,1,2,0:T(1,128)} %param.10) | copy-start | bytes 589828
  2.2 0.7 %copy-start.2 = (f32[1,1,12,256]{3,1,2,0:T(1,128)S(1)}, f32[1,1,12,256]{3,1,2,0:T(1,128)}, u32[]{:S(2)}) copy-start(f32[1,1,12,256]{3,1,2,0:T(1,128)} %param.14) | copy-start | bytes 36868
  2.9 0.7 %copy-start.3 = (s32[1,1,12,2]{2,3,1,0:T(2,128)S(1)}, s32[1,1,12,2]{2,3,1,0:T(2,128)}, u32[]{:S(2)}) copy-start(s32[1,1,12,2]{2,3,1,0:T(2,128)} %param.11) | copy-start | bytes 292
  3.6 0.7 %copy-start.6 = (s32[1,1,12]{2,1,0:T(1,128)S(1)}, s32[1,1,12]{2,1,0:T(1,128)}, u32[]{:S(2)}) copy-start(s32[1,1,12]{2,1,0:T(1,128)} %param.12) | copy-start | bytes 148
  4.6 9.4 %collective-permute-start = (f32[8,6656]{1,0:T(8,128)S(1)}, f32[8,6656]{1,0:T(8,128)S(1)}, u32[]{:S(2)}, u32[]{:S(2)}) collective-permute-start(f32[8,6656]{1,0:T(8,128)S(1)} %pack.1.after_ref.own_ref), channel_id=1, source_target_pairs={{0,1},{1,2},{2,3},{3,4},{4,5},{5,6},{6,7},{7,8},{8,9},{9,10},{10,1... | collective-permute-start | bytes 638984 | tf_op jit(solution)/shard_map/ppermute | solution.py:425
  9.5 8.4 %collective-permute-start.1 = (f32[8,6656]{1,0:T(8,128)S(1)}, f32[8,6656]{1,0:T(8,128)S(1)}, u32[]{:S(2)}, u32[]{:S(2)}) collective-permute-start(f32[8,6656]{1,0:T(8,128)S(1)} %pack.1.after_ref.own_ref), channel_id=1, source_target_pairs={{0,16},{1,17},{2,18},{3,19},{4,20},{5,21},{6,22},{7,23},{8,24},{9,... | collective-permute-start | bytes 638984 | tf_op jit(solution)/shard_map/ppermute | solution.py:425
  13.9 4.0 %collective-permute-start.2 = (f32[8,6656]{1,0:T(8,128)S(1)}, f32[8,6656]{1,0:T(8,128)S(1)}, u32[]{:S(2)}, u32[]{:S(2)}) collective-permute-start(f32[8,6656]{1,0:T(8,128)S(1)} %collective-permute-done.west_ref), channel_id=1, source_target_pairs={{0,16},{1,17},{2,18},{3,19},{4,20},{5,21},{6,22},{7,23},{8,24},{9,... | collective-permute-start | bytes 638984 | tf_op jit(solution)/shard_map/ppermute | solution.py:425
  16.1 1.6 %copy-start = (bf16[64,64,256]{2,1,0:T(8,128)(2,1)S(1)}, bf16[64,64,256]{2,1,0:T(8,128)(2,1)}, u32[]{:S(2)}) copy-start(bf16[64,64,256]{2,1,0:T(8,128)(2,1)} %param.9) | copy-start | bytes 6291460
  17.7 0.7 %copy-start.5 = (f32[2,256]{1,0:T(2,128)S(1)}, f32[2,256]{1,0:T(2,128)}, u32[]{:S(2)}) copy-start(f32[2,256]{1,0:T(2,128)} %back_trace_ref.3) | copy-start | bytes 6148
  17.9 2.6 %copy-start.7 = (s32[2]{0:T(128)S(1)}, s32[2]{0:T(128)}, u32[]{:S(2)}) copy-start(s32[2]{0:T(128)} %window_ref.1) | copy-start | bytes 28
  22.9 8.9 %collective-permute-start.3 = (f32[16,6144]{1,0:T(8,128)S(1)}, f32[16,6144]{1,0:T(8,128)S(1)}, u32[]{:S(2)}, u32[]{:S(2)}) collective-permute-start(f32[16,6144]{1,0:T(8,128)S(1)} %get-tuple-element.15), channel_id=1, source_target_pairs={{16,0},{17,1},{18,2},{19,3},{20,4},{21,5},{22,6},{23,7},{24,8},{25... | collective-permute-start | bytes 1179656 | tf_op jit(solution)/shard_map/ppermute | solution.py:425
  24.2 21.6 %all-to-all-start = ((f32[32,24,128]{2,1,0:T(8,128)}), f32[32,24,128]{2,1,0:T(8,128)S(1)}, u32[]{:S(2)}, u32[]{:S(2)}) async-start(f32[32,24,128]{2,1,0:T(8,128)} %get-tuple-element.17), calls=%async_computation | async-start | bytes 786432 | tf_op jit(solution)/shard_map/all_to_all | solution.py:508
  31.8 26.3 %copy-start.4 = (s32[1,1,12,2]{2,3,1,0:T(2,128)S(1)}, s32[1,1,12,2]{2,3,1,0:T(2,128)}, u32[]{:S(2)}) copy-start(s32[1,1,12,2]{2,3,1,0:T(2,128)} %param.11) | copy-start | bytes 292
  31.8 19.1 %collective-permute-start.4 = (f32[8,6144]{1,0:T(8,128)S(1)}, f32[8,6144]{1,0:T(8,128)S(1)}, u32[]{:S(2)}, u32[]{:S(2)}) collective-permute-start(f32[8,6144]{1,0:T(8,128)S(1)} %slice_add_fusion), channel_id=1, source_target_pairs={{1,0},{2,1},{3,2},{4,3},{5,4},{6,5},{7,6},{8,7},{9,8},{10,9},{11,1... | collective-permute-start | bytes 589832 | tf_op jit(solution)/shard_map/ppermute | solution.py:425
  48.4 9.6 %all-to-all-start.1 = ((f32[32,1,128]{2,1,0:T(1,128)}), f32[32,1,128]{2,1,0:T(1,128)S(1)}, u32[]{:S(2)}, u32[]{:S(2)}) async-start(f32[32,1,128]{2,1,0:T(1,128)} %bitcast.7), calls=%async_computation.1 | async-start | bytes 32768 | tf_op jit(solution)/shard_map/all_to_all | solution.py:523
